TPU v7x, 16 devices: a whole 2x2x2 slice. The times are simulated.
16 devices in a mesh: dp: 2 (over z), fsdp: 8 (over y, x, core).
Axes of the slice: x: 2, y: 2, z: 2, core: 2. Of those that a mesh axis runs over, the one named last changes fastest.
Arguments:
- emb_grad: float32 [2, 8, 2048, 5376], P('dp', 'fsdp')
- mat_grad: float32 [2, 8, 1024, 5376], P('dp', 'fsdp')
- norm_grad: float32 [2, 8, 9, 5376], P('dp', 'fsdp')
- emb_param: float32 [2048, 5376], P('fsdp')
- emb_mom: float32 [2048, 5376], P('fsdp')
- emb_var: float32 [2048, 5376], P('fsdp')
- mat_param: float32 [1024, 5376], P('fsdp')
- mat_mom: float32 [1024, 5376], P('fsdp')
- mat_var: float32 [1024, 5376], P('fsdp')
- norm_param: float32 [9, 5376], P(None, 'fsdp')
- norm_mom: float32 [9, 5376], P(None, 'fsdp')
- norm_var: float32 [9, 5376], P(None, 'fsdp')
Outputs:
- output 1: float32 [2048, 5376], P('fsdp')
- output 2: float32 [2048, 5376], P('fsdp')
- output 3: float32 [2048, 5376], P('fsdp')
- output 4: bfloat16 [2048, 5376], P('fsdp')
- output 5: float32 [1024, 5376], P('fsdp')
- output 6: float32 [1024, 5376], P('fsdp')
- output 7: float32 [1024, 5376], P('fsdp')
- output 8: bfloat16 [1024, 5376], P('fsdp')
- output 9: float32 [9, 5376], P(None, 'fsdp')
- output 10: float32 [9, 5376], P(None, 'fsdp')
- output 11: float32 [9, 5376], P(None, 'fsdp')
- output 12: bfloat16 [9, 5376], P(None, 'fsdp')
All inputs are finite; a program needn't handle non-finite values.
Results may differ from a plain program's by a relative error of at most 0.001.
Values sent between devices are 32-bit elements.
A program may use at most 1 GiB of HBM per device.

v0:
```python
import jax
import jax.numpy as jnp
from jax import lax
from jax.sharding import PartitionSpec as P

LEARN_RATE = 0.003
BETA_ONE = 0.9
BETA_TWO = 0.95
ADAM_EPS = 1e-8
WEIGHT_DECAY = 0.1
CLIP_NORM = 1.0
ADAM_STEP = 10


def adamw_update(grad_part, param_old, mom_old, var_old, decay_rate):
    new_mom = BETA_ONE * mom_old + (1.0 - BETA_ONE) * grad_part
    new_var = BETA_TWO * var_old + (1.0 - BETA_TWO) * grad_part * grad_part
    mom_hat = new_mom / (1.0 - BETA_ONE ** ADAM_STEP)
    var_hat = new_var / (1.0 - BETA_TWO ** ADAM_STEP)
    step_dir = mom_hat / (jnp.sqrt(var_hat) + ADAM_EPS)
    new_param = param_old - LEARN_RATE * (step_dir + decay_rate * param_old)
    return (new_param, new_mom, new_var, new_param.astype(jnp.bfloat16))


def solution(mesh):
    dev_count = mesh.shape["dp"] * mesh.shape["fsdp"]

    def local_step(emb_grad, mat_grad, norm_grad, emb_param, emb_mom, emb_var, mat_param, mat_mom, mat_var, norm_param, norm_mom, norm_var):
        emb_part = lax.psum_scatter(emb_grad[0, 0], "fsdp", scatter_dimension=0, tiled=True)
        mat_part = lax.psum_scatter(mat_grad[0, 0], "fsdp", scatter_dimension=0, tiled=True)
        norm_part = lax.psum_scatter(norm_grad[0, 0], "fsdp", scatter_dimension=1, tiled=True)
        emb_mean = lax.psum(emb_part, "dp") / dev_count
        mat_mean = lax.psum(mat_part, "dp") / dev_count
        norm_mean = lax.psum(norm_part, "dp") / dev_count
        local_sq = jnp.sum(emb_mean * emb_mean) + jnp.sum(mat_mean * mat_mean) + jnp.sum(norm_mean * norm_mean)
        total_sq = lax.psum(local_sq, "fsdp")
        clip_scale = jnp.minimum(1.0, CLIP_NORM / jnp.sqrt(total_sq))
        emb_out = adamw_update(emb_mean * clip_scale, emb_param, emb_mom, emb_var, WEIGHT_DECAY)
        mat_out = adamw_update(mat_mean * clip_scale, mat_param, mat_mom, mat_var, WEIGHT_DECAY)
        norm_out = adamw_update(norm_mean * clip_scale, norm_param, norm_mom, norm_var, 0.0)
        return emb_out + mat_out + norm_out

    grad_spec = P("dp", "fsdp", None, None)
    row_spec = P("fsdp", None)
    col_spec = P(None, "fsdp")
    in_list = (grad_spec, grad_spec, grad_spec, row_spec, row_spec, row_spec, row_spec, row_spec, row_spec, col_spec, col_spec, col_spec)
    out_list = (row_spec, row_spec, row_spec, row_spec, row_spec, row_spec, row_spec, row_spec, col_spec, col_spec, col_spec, col_spec)
    return jax.shard_map(local_step, mesh=mesh, in_specs=in_list, out_specs=out_list, check_vma=False)
```

profile of v0, /device:TPU:0, one launch (start us, length us, event | category | flops | bytes accessed | tf_op | source)
XLA Modules:
  0.0 686.0 jit_solution(9824221636126662262)
XLA Ops:
  7.2 0.0 reduce-scatter.8.cloned.1.call-start
  7.2 0.7 reduce-scatter.8.cloned.1.call-update
  7.9 0.0 reduce-scatter.6.cloned.1.call-start
  8.0 0.0 copy-start.4
  8.0 0.7 reduce-scatter.6.cloned.1.call-update
  8.7 0.0 reduce-scatter.10.cloned.1.call-start
  8.7 0.2 copy-done.4
  8.9 2.0 copy.26
  10.9 0.0 reduce-scatter.10.cloned.1.call-update
  10.9 0.0 all-reduce.3.cloned.1.call-start
  11.0 137.7 %reduce-scatter.8.cloned.1.call-done = f32[128,5376]{1,0:T(8,128)} async-done(((f32[1024,5376]{1,0:T(8,128)}), f32[128,5376]{1,0:T(8,128)}) %reduce-scatter.8.cloned.1.call-update) | async-done | bytes 2752528 | tf_op jit(solution)/shard_map/reduce_scatter | solution.py:30
  148.7 251.3 %reduce-scatter.6.cloned.1.call-done = f32[256,5376]{1,0:T(8,128)} async-done(((f32[2048,5376]{1,0:T(8,128)}), f32[256,5376]{1,0:T(8,128)}) %reduce-scatter.6.cloned.1.call-update) | async-done | bytes 5505040 | tf_op jit(solution)/shard_map/reduce_scatter | solution.py:29
  400.0 0.0 all-reduce.3.cloned.1.call-update
  400.0 42.2 %reduce-scatter.10.cloned.1.call-done = f32[672,9]{1,0:T(8,128)} async-done(((f32[5376,9]{1,0:T(8,128)}), f32[672,9]{1,0:T(8,128)}) %reduce-scatter.10.cloned.1.call-update) | async-done | bytes 24208
  442.2 1.1 copy.25
  443.3 9.3 %psum.30 = f32[9,672]{1,0:T(8,128)S(1)} all-reduce(f32[9,672]{1,0:T(8,128)S(1)} %copy.25), channel_id=1, replica_groups=mesh['dp'=2,'fsdp'=8] {'dp'}, use_global_device_ids=true, to_apply=%region_7.0 | all-reduce | flops 6048 | bytes 48384 | tf_op jit(solution)/shard_map/psum | solution.py:34
  452.6 0.6 multiply_reduce_fusion.2
  453.2 182.8 %all-reduce.3.cloned.1.call-done = (f32[256,5376]{1,0:T(8,128)}, f32[128,5376]{1,0:T(8,128)}) async-done(((f32[256,5376]{1,0:T(8,128)}, f32[128,5376]{1,0:T(8,128)}), (f32[256,5376]{1,0:T(8,128)}, f32[128,5376]{1,0:T(8,128)})) %all-reduce.3.cloned.1.call-update) | async-done | bytes 8257552 | tf_op jit(solution)/shard_map/psum | solution.py:32
  636.0 0.0 copy-start
  636.0 4.7 multiply_reduce_fusion
  640.8 0.0 copy-done
  640.8 1.3 multiply_reduce_fusion.1
  644.0 13.8 %psum.31 = f32[]{:T(128)} all-reduce(f32[]{:T(128)S(6)} %add.66), channel_id=1, replica_groups=mesh['dp'=2,'fsdp'=8] {'fsdp'}, use_global_device_ids=true, to_apply=%region_9.0 | all-reduce | flops 1 | bytes 8 | tf_op jit(solution)/shard_map/psum | solution.py:36
  658.6 0.0 copy-start.1
  658.6 0.0 copy-start.2
  658.6 0.0 copy-start.3
  658.6 15.8 %fusion.7 = (bf16[256,5376]{1,0:T(8,128)(2,1)}, f32[256,5376]{1,0:T(8,128)}, f32[256,5376]{1,0:T(8,128)}, f32[256,5376]{1,0:T(8,128)}) fusion(f32[256,5376]{1,0:T(8,128)} %param.15, f32[256,5376]{1,0:T(8,128)} %get-tuple-element.12, f32[]{:T(128)S(6)} %mul.139, f32[256,5376]{1,0:T(8,128)} %param.16, f32[256,5376]{1,0:T(8,128)} %param.17), kind=kLoop, calls=%fused_computation.17 | loop fusion | flops 23396352 | bytes 41287684 | tf_op jit(solution)/shard_map/convert_element_type | solution.py:22
  674.4 0.0 copy-done.1
  674.4 0.0 copy-done.2
  674.4 0.0 copy-done.3
  674.4 0.0 copy-start.5
  674.4 0.0 copy-start.6
  674.4 0.0 copy-start.7
  674.4 4.4 fusion.5
  678.8 0.0 copy-done.5
  678.8 0.0 copy-done.6
  678.8 0.0 copy-done.7
  678.8 0.7 fusion.3
Async XLA Ops:
  7.2 141.5 %reduce-scatter.8.cloned.1.call-start = ((), (), s32[]{:S(2)}) async-start(), calls=%async_computation.4 | async-start | bytes 24772608 | tf_op jit(solution)/shard_map/reduce_scatter | solution.py:30
  7.9 392.1 %reduce-scatter.6.cloned.1.call-start = ((), (), s32[]{:S(2)}) async-start(), calls=%async_computation.3 | async-start | bytes 49545216 | tf_op jit(solution)/shard_map/reduce_scatter | solution.py:29
  8.0 0.9 copy-start.4
  8.7 433.5 %reduce-scatter.10.cloned.1.call-start = ((), (), s32[]{:S(2)}) async-start(), calls=%async_computation.5 | async-start | bytes 3096576
  10.9 625.1 %all-reduce.3.cloned.1.call-start = ((), (), s32[]{:S(2)}) async-start(), calls=%async_computation.6 | async-start | bytes 16515072 | tf_op jit(solution)/shard_map/psum | solution.py:32
  636.0 4.7 copy-start
  658.6 15.8 %copy-start.1 = (f32[128,5376]{1,0:T(8,128)S(1)}, f32[128,5376]{1,0:T(8,128)}, u32[]{:S(2)}) copy-start(f32[128,5376]{1,0:T(8,128)} %param.18) | copy-start | bytes 8257540
  658.6 15.8 %copy-start.2 = (f32[128,5376]{1,0:T(8,128)S(1)}, f32[128,5376]{1,0:T(8,128)}, u32[]{:S(2)}) copy-start(f32[128,5376]{1,0:T(8,128)} %param.19) | copy-start | bytes 8257540
  658.6 15.8 %copy-start.3 = (f32[128,5376]{1,0:T(8,128)S(1)}, f32[128,5376]{1,0:T(8,128)}, u32[]{:S(2)}) copy-start(f32[128,5376]{1,0:T(8,128)} %param.20) | copy-start | bytes 8257540
  674.4 4.4 copy-start.5
  674.4 4.4 copy-start.6
  674.4 4.4 copy-start.7
Sparse Core Ops, SparseCore 0:
  11.6 137.0 reduce-scatter.7
  152.4 247.5 reduce-scatter.5
  403.9 38.2 reduce-scatter.9
  444.5 191.4 all-reduce.2
where the time goes:
time: 686 us
  waiting for transfers between devices  615 us (90%)
  other arithmetic  27.5 us (4%)
  blocking collectives  23.1 us (3%)
  between operations  16.5 us (2%)
    reduce_scatter x1, waiting for transfers between devices, local_step(): lax.psum_scatter(emb_grad[0, 0], 'fsdp', scatter_dimension=0, tiled=True)  251 us
    psum x1, waiting for transfers between devices, local_step(): emb_mean = lax.psum(emb_part, 'dp') / dev_count  183 us
    reduce_scatter x1, waiting for transfers between devices, local_step(): lax.psum_scatter(mat_grad[0, 0], 'fsdp', scatter_dimension=0, tiled=True)  138 us
    unnamed x5, waiting for transfers between devices  43.6 us
    convert_element_type x3, other arithmetic, adamw_update(): return (new_param, new_mom, new_var, new_param.astype(jnp.bfloat16))  20.8 us
    psum x1, blocking collectives, local_step(): total_sq = lax.psum(local_sq, 'fsdp')  13.8 us
  transfers between devices with their start and end apart: 4, of which 4 were waited for; matrix products, arithmetic and copies ran while one was open for 1% of the time, Pallas kernels for 0%

commit v1 on v0

v1 whole, which is shorter than its diff:
```python
import functools

import jax
import jax.numpy as jnp
from jax import lax
from jax.experimental import pallas as pl
from jax.experimental.pallas import tpu as pltpu
from jax.sharding import PartitionSpec as P

LEARN_RATE = 0.003
BETA_ONE = 0.9
BETA_TWO = 0.95
ADAM_EPS = 1e-8
WEIGHT_DECAY = 0.1
CLIP_NORM = 1.0
ADAM_STEP = 10

MESH = pl.DeviceIdType.MESH
F32 = jnp.float32

WIDTH = 5376
NORM_ROWS = 9
NORM_COLS = 672
NORM_PAD = (16, 768)
ROWS = 8
SPLIT = 2688
LAG_ZERO = 3
LAG = 2
P_SLOTS = 8
R_SLOTS = 6
SEND_SLOTS = 8


def reduce_kernel(counts, emb, mat, norm, emb_out, mat_out, norm_out, scale_out,
                  part, recv_zero, xa, xb, ya, yb, grad, square,
                  norm_in, norm_part, norm_a, norm_b, norm_c, norm_d, sum_send, sum_recv,
                  load_sem, zero_send, zero_recv, credit,
                  a_send, b_send, xa_recv, xb_recv, ya_send, yb_send, ya_recv, yb_recv,
                  za_send, zb_send, za_recv, zb_recv, out_sem,
                  norm_load, norm_send, norm_recv, norm_store, sum_ssem, sum_rsem, scale_sem):
    emb_count, mat_count = counts
    total = emb_count + mat_count
    z = lax.axis_index("dp")
    f = lax.axis_index("fsdp")
    c = lax.rem(f, 2)
    x = lax.rem(lax.div(f, 2), 2)
    y = lax.div(f, 4)
    core = (z, f + 1 - 2 * c)
    xn = (z, f + 2 - 4 * x)
    yn = (z, f + 4 - 8 * y)
    zn = (1 - z, f)

    def remote(src, dst, ssem, rsem, dev):
        return pltpu.make_async_remote_copy(src_ref=src, dst_ref=dst, send_sem=ssem, recv_sem=rsem,
                                            device_id=dev, device_id_type=MESH)

    barrier = pltpu.get_barrier_semaphore()
    for dev in (core, xn, yn, zn):
        pl.semaphore_signal(barrier, inc=1, device_id=dev, device_id_type=MESH)
    norm_copy = pltpu.make_async_copy(norm, norm_in, norm_load)
    norm_copy.start()
    norm_part[...] = jnp.zeros_like(norm_part)
    square[...] = jnp.zeros_like(square)
    norm_copy.wait()
    for k in range(8):
        norm_part[k // 4, (k // 2) % 2, k % 2, :NORM_ROWS, :NORM_COLS] = norm_in[:, k * NORM_COLS:(k + 1) * NORM_COLS]
    pl.semaphore_wait(barrier, 4)

    def on_rows(j, body):
        @pl.when(j < emb_count)
        def _():
            body(emb, emb_out, pl.multiple_of(j * ROWS, ROWS))

        @pl.when(j >= emb_count)
        def _():
            body(mat, mat_out, pl.multiple_of((j - emb_count) * ROWS, ROWS))

    def load_copy(ref, row, j):
        return pltpu.make_async_copy(ref.at[:, :, c, pl.ds(row, ROWS), :], part.at[lax.rem(j, P_SLOTS)],
                                     load_sem.at[lax.rem(j, P_SLOTS)])

    def zero_copy(ref, row, j):
        return remote(ref.at[:, :, 1 - c, pl.ds(row, ROWS), :], recv_zero.at[lax.rem(j, R_SLOTS)],
                      zero_send.at[lax.rem(j, R_SLOTS)], zero_recv.at[lax.rem(j, R_SLOTS)], core)

    def a_one(j):
        s = lax.rem(j, P_SLOTS)
        return remote(part.at[s, :, 1 - x, :, :SPLIT], xa.at[j], a_send.at[s], xa_recv.at[j], xn)

    def b_one(j):
        s = lax.rem(j, P_SLOTS)
        return remote(part.at[s, 1 - y, :, :, SPLIT:], xb.at[j], b_send.at[s], xb_recv.at[j], yn)

    def a_two(j):
        s = lax.rem(j, SEND_SLOTS)
        return remote(xa.at[j, 1 - y], ya.at[j], ya_send.at[s], ya_recv.at[j], yn)

    def b_two(j):
        s = lax.rem(j, SEND_SLOTS)
        return remote(xb.at[j, 1 - x], yb.at[j], yb_send.at[s], yb_recv.at[j], xn)

    def a_three(j):
        s = lax.rem(j, SEND_SLOTS)
        return remote(ya.at[j], grad.at[j, :, :SPLIT], za_send.at[s], za_recv.at[j], zn)

    def b_three(j):
        s = lax.rem(j, SEND_SLOTS)
        return remote(yb.at[j], grad.at[j, :, SPLIT:], zb_send.at[s], zb_recv.at[j], zn)

    def out_copy(ref, row, j):
        return pltpu.make_async_copy(grad.at[j], ref.at[pl.ds(row, ROWS), :], out_sem.at[lax.rem(j, SEND_SLOTS)])

    norm_zero = remote(norm_part.at[:, :, 1 - c], norm_a, norm_send.at[0], norm_recv.at[0], core)
    norm_one = remote(norm_a.at[:, 1 - x], norm_b, norm_send.at[1], norm_recv.at[1], xn)
    norm_two = remote(norm_b.at[1 - y], norm_c, norm_send.at[2], norm_recv.at[2], yn)
    norm_three = remote(norm_c, norm_d, norm_send.at[3], norm_recv.at[3], zn)
    norm_zero.start()

    def when_in(j, body):
        pl.when(jnp.logical_and(j >= 0, j < total))(functools.partial(body, j))

    def stage_issue(j):
        @pl.when(j >= P_SLOTS)
        def _():
            a_one(j - P_SLOTS).wait_send()
            b_one(j - P_SLOTS).wait_send()

        @pl.when(j >= R_SLOTS)
        def _():
            zero_copy(emb, 0, j - R_SLOTS).wait_send()
            pl.semaphore_wait(credit, 1)

        def body(ref, _, row):
            zero_copy(ref, row, j).start()
            load_copy(ref, row, j).start()

        on_rows(j, body)

    def stage_one(j):
        load_copy(emb, 0, j).wait()
        zero_copy(emb, 0, j).wait_recv()
        s = lax.rem(j, P_SLOTS)
        part[s] += recv_zero[lax.rem(j, R_SLOTS)]

        @pl.when(j + R_SLOTS < total)
        def _():
            pl.semaphore_signal(credit, inc=1, device_id=core, device_id_type=MESH)

        a_one(j).start()
        b_one(j).start()

    def stage_two(j):
        s = lax.rem(j, P_SLOTS)
        a_one(j).wait_recv()
        xa[j] += part[s, :, x, :, :SPLIT]
        b_one(j).wait_recv()
        xb[j] += part[s, y, :, :, SPLIT:]

        @pl.when(j >= SEND_SLOTS)
        def _():
            a_two(j - SEND_SLOTS).wait_send()
            b_two(j - SEND_SLOTS).wait_send()

        a_two(j).start()
        b_two(j).start()

    def stage_three(j):
        a_two(j).wait_recv()
        ya[j] += xa[j, y]
        b_two(j).wait_recv()
        yb[j] += xb[j, x]

        @pl.when(j >= SEND_SLOTS)
        def _():
            a_three(j - SEND_SLOTS).wait_send()
            b_three(j - SEND_SLOTS).wait_send()

        a_three(j).start()
        b_three(j).start()

    def stage_four(j):
        a_three(j).wait_recv()
        b_three(j).wait_recv()
        left = (grad[j, :, :SPLIT] + ya[j]) * (1.0 / 16.0)
        right = (grad[j, :, SPLIT:] + yb[j]) * (1.0 / 16.0)
        grad[j, :, :SPLIT] = left
        grad[j, :, SPLIT:] = right
        square[:, :SPLIT] += left * left
        square[:, SPLIT:] += right * right

        @pl.when(j >= SEND_SLOTS)
        def _():
            out_copy(emb_out, 0, j - SEND_SLOTS).wait()

        def body(_, ref, row):
            out_copy(ref, row, j).start()

        on_rows(j, body)

    def trip(it, carry):
        when_in(it, stage_issue)
        when_in(it - LAG_ZERO, stage_one)
        when_in(it - LAG_ZERO - LAG, stage_two)
        when_in(it - LAG_ZERO - 2 * LAG, stage_three)
        when_in(it - LAG_ZERO - 3 * LAG, stage_four)

        @pl.when(it == 4)
        def _():
            norm_zero.wait_recv()
            norm_a[...] += norm_part[:, :, c]
            norm_one.start()

        @pl.when(it == 8)
        def _():
            norm_one.wait_recv()
            norm_b[...] += norm_a[:, x]
            norm_two.start()

        @pl.when(it == 12)
        def _():
            norm_two.wait_recv()
            norm_c[...] += norm_b[y]
            norm_three.start()

        @pl.when(it == 16)
        def _():
            norm_three.wait_recv()
            norm_d[...] = (norm_d[...] + norm_c[...]) * (1.0 / 16.0)
            pltpu.make_async_copy(norm_d, norm_out, norm_store).start()

        return carry

    lax.fori_loop(0, total + LAG_ZERO + 3 * LAG, trip, 0)

    norm_sq = norm_d[...] * norm_d[...]
    local = jnp.sum(square[...]) + jnp.sum(norm_sq)
    value = jnp.full((8, 128), local, F32)
    for k, dev in enumerate((core, xn, yn)):
        sum_send[k] = value
        copy = remote(sum_send.at[k], sum_recv.at[k], sum_ssem.at[k], sum_rsem.at[k], dev)
        copy.start()
        copy.wait_recv()
        value = value + sum_recv[k]
    sum_send[3] = jnp.minimum(1.0, CLIP_NORM / jnp.sqrt(value))
    scale_copy = pltpu.make_async_copy(sum_send.at[3], scale_out, scale_sem)
    scale_copy.start()

    for k, dev in enumerate((core, xn, yn)):
        remote(sum_send.at[k], sum_recv.at[k], sum_ssem.at[k], sum_rsem.at[k], dev).wait_send()
    for copy in (norm_zero, norm_one, norm_two, norm_three):
        copy.wait_send()
    pltpu.make_async_copy(norm_d, norm_out, norm_store).wait()

    def drain(slots, copies):
        def body(j, carry):
            for copy in copies:
                copy(j).wait_send()
            return carry
        lax.fori_loop(total - slots, total, body, 0)

    drain(P_SLOTS, (a_one, b_one))
    drain(R_SLOTS, (functools.partial(zero_copy, emb, 0),))
    drain(SEND_SLOTS, (a_two, b_two, a_three, b_three))

    def last(j, carry):
        out_copy(emb_out, 0, j).wait()
        return carry

    lax.fori_loop(total - SEND_SLOTS, total, last, 0)
    scale_copy.wait()


def reduce_grads(emb_grad, mat_grad, norm_grad):
    emb_rows = emb_grad.shape[0] // 8
    mat_rows = mat_grad.shape[0] // 8
    counts = (emb_rows // ROWS, mat_rows // ROWS)
    total = sum(counts)
    dma = pltpu.SemaphoreType.DMA
    scratch = [
        pltpu.VMEM((P_SLOTS, 2, 2, ROWS, WIDTH), F32),
        pltpu.VMEM((R_SLOTS, 2, 2, ROWS, WIDTH), F32),
        pltpu.VMEM((total, 2, ROWS, SPLIT), F32),
        pltpu.VMEM((total, 2, ROWS, WIDTH - SPLIT), F32),
        pltpu.VMEM((total, ROWS, SPLIT), F32),
        pltpu.VMEM((total, ROWS, WIDTH - SPLIT), F32),
        pltpu.VMEM((total, ROWS, WIDTH), F32),
        pltpu.VMEM((ROWS, WIDTH), F32),
        pltpu.VMEM((NORM_ROWS, WIDTH), F32),
        pltpu.VMEM((2, 2, 2) + NORM_PAD, F32),
        pltpu.VMEM((2, 2) + NORM_PAD, F32),
        pltpu.VMEM((2,) + NORM_PAD, F32),
        pltpu.VMEM(NORM_PAD, F32),
        pltpu.VMEM(NORM_PAD, F32),
        pltpu.VMEM((4, 8, 128), F32),
        pltpu.VMEM((3, 8, 128), F32),
        dma((P_SLOTS,)), dma((R_SLOTS,)), dma((R_SLOTS,)), pltpu.SemaphoreType.REGULAR,
        dma((P_SLOTS,)), dma((P_SLOTS,)), dma((total,)), dma((total,)),
        dma((SEND_SLOTS,)), dma((SEND_SLOTS,)), dma((total,)), dma((total,)),
        dma((SEND_SLOTS,)), dma((SEND_SLOTS,)), dma((total,)), dma((total,)), dma((SEND_SLOTS,)),
        dma, dma((4,)), dma((4,)), dma, dma((3,)), dma((3,)), dma,
    ]
    hbm = pl.BlockSpec(memory_space=pl.ANY)
    return pl.pallas_call(
        functools.partial(reduce_kernel, counts),
        out_shape=(
            jax.ShapeDtypeStruct((emb_rows, WIDTH), F32),
            jax.ShapeDtypeStruct((mat_rows, WIDTH), F32),
            jax.ShapeDtypeStruct(NORM_PAD, F32),
            jax.ShapeDtypeStruct((8, 128), F32),
        ),
        in_specs=[hbm] * 3,
        out_specs=(hbm,) * 4,
        scratch_shapes=scratch,
        compiler_params=pltpu.CompilerParams(
            collective_id=0, has_side_effects=True, vmem_limit_bytes=50 * 1024 * 1024
        ),
        name="reduce_grads",
    )(emb_grad.reshape(2, 2, 2, emb_rows, WIDTH), mat_grad.reshape(2, 2, 2, mat_rows, WIDTH), norm_grad)


def adamw_update(grad_part, param_old, mom_old, var_old, decay_rate):
    new_mom = BETA_ONE * mom_old + (1.0 - BETA_ONE) * grad_part
    new_var = BETA_TWO * var_old + (1.0 - BETA_TWO) * grad_part * grad_part
    mom_hat = new_mom / (1.0 - BETA_ONE ** ADAM_STEP)
    var_hat = new_var / (1.0 - BETA_TWO ** ADAM_STEP)
    step_dir = mom_hat / (jnp.sqrt(var_hat) + ADAM_EPS)
    new_param = param_old - LEARN_RATE * (step_dir + decay_rate * param_old)
    return (new_param, new_mom, new_var, new_param.astype(jnp.bfloat16))


def solution(mesh):
    def local_step(emb_grad, mat_grad, norm_grad, emb_param, emb_mom, emb_var, mat_param, mat_mom, mat_var, norm_param, norm_mom, norm_var):
        emb_mean, mat_mean, norm_mean, scale = reduce_grads(emb_grad[0, 0], mat_grad[0, 0], norm_grad[0, 0])
        clip_scale = scale[0, 0]
        emb_out = adamw_update(emb_mean * clip_scale, emb_param, emb_mom, emb_var, WEIGHT_DECAY)
        mat_out = adamw_update(mat_mean * clip_scale, mat_param, mat_mom, mat_var, WEIGHT_DECAY)
        norm_out = adamw_update(norm_mean[:NORM_ROWS, :NORM_COLS] * clip_scale, norm_param, norm_mom, norm_var, 0.0)
        return emb_out + mat_out + norm_out

    grad_spec = P("dp", "fsdp", None, None)
    row_spec = P("fsdp", None)
    col_spec = P(None, "fsdp")
    in_list = (grad_spec, grad_spec, grad_spec, row_spec, row_spec, row_spec, row_spec, row_spec, row_spec, col_spec, col_spec, col_spec)
    out_list = (row_spec, row_spec, row_spec, row_spec, row_spec, row_spec, row_spec, row_spec, col_spec, col_spec, col_spec, col_spec)
    return jax.shard_map(local_step, mesh=mesh, in_specs=in_list, out_specs=out_list, check_vma=False)
```

time: 686 us -> 317 us (0.46)
  waiting for transfers between devices: 615 us -> 0 us
  Pallas kernels: 0 us -> 295 us
  blocking collectives: 23.1 us -> 0 us
  between operations: 16.5 us -> 0.73 us
  other arithmetic: 27.5 us -> 19.7 us
    reduce_scatter x2 -> x0, waiting for transfers between devices: 389 us -> none  [the longest x1 251 us: local_step(): lax.psum_scatter(emb_grad[0, 0], 'fsdp', scatter_dimension=0, tiled=True)]
    pallas_call x0 -> x1, Pallas kernels: none -> 295 us  [reduce_grads(): pl.pallas_call(functools.partial(reduce_kernel, counts), out_shape=(jax.S...]
    psum x1 -> x0, waiting for transfers between devices: 183 us -> none  [local_step(): emb_mean = lax.psum(emb_part, 'dp') / dev_count]
    unnamed x5 -> x0, waiting for transfers between devices: 43.6 us -> none
    psum x2 -> x0, blocking collectives: 23.1 us -> none  [the longest x1 13.8 us: local_step(): total_sq = lax.psum(local_sq, 'fsdp')]
  transfers between devices with their start and end apart: 4 -> 0, of which waited for: 4 -> 0; matrix products, arithmetic and copies ran while one was open for 1% -> 0% of each run, Pallas kernels for 0% -> 0%
where the time goes in v1:
time: 317 us
  Pallas kernels  295 us (93%)
  other arithmetic  19.7 us (6%)
    pallas_call x1, Pallas kernels, reduce_grads(): pl.pallas_call(functools.partial(reduce_kernel, counts), out_shape=(jax.S...  295 us
    convert_element_type x3, other arithmetic, adamw_update(): return (new_param, new_mom, new_var, new_param.astype(jnp.bfloat16))  19.7 us

profile of v1, /device:TPU:0, one launch (start us, length us, event | category | flops | bytes accessed | tf_op | source)
XLA Modules:
  0.0 317.0 jit_solution(7148396906477342716)
XLA Ops:
  0.6 1.0 copy.26
  1.6 0.0 slice-start
  1.6 0.0 slice-start.2
  1.6 0.0 slice-start.1
  1.6 0.0 slice-start.3
  1.6 295.0 %reduce_grads.1 = (f32[256,5376]{1,0:T(8,128)}, f32[128,5376]{1,0:T(8,128)S(1)}, f32[16,768]{1,0:T(8,128)S(1)}, f32[8,128]{1,0:T(8,128)S(1)}) custom-call(f32[2,2,2,256,5376]{4,3,2,1,0:T(8,128)} %bitcast.7, f32[2,2,2,128,5376]{4,3,2,1,0:T(8,128)} %bitcast.8, f32[9,5376]{1,0:T(8,128)S(1)} %bitcast.6), custom_call_target="tpu_custom_call" | custom-call | tf_op jit(solution)/shard_map/reduce_grads/pallas_call | solution.py:303
  296.7 0.5 slice.6
  297.2 0.0 slice-done
  297.2 0.0 slice-done.2
  297.2 0.0 slice-done.1
  297.2 0.0 slice-done.3
  297.2 11.3 %fusion.7 = (bf16[256,5376]{1,0:T(8,128)(2,1)}, f32[256,5376]{1,0:T(8,128)}, f32[256,5376]{1,0:T(8,128)}, f32[256,5376]{1,0:T(8,128)}) fusion(f32[256,5376]{1,0:T(8,128)S(1)} %bitcast.10, f32[256,5376]{1,0:T(8,128)} %get-tuple-element.16, f32[]{:T(128)} %bitcast.2, f32[256,5376]{1,0:T(8,128)S(1)} %bitcast.12, f32[256,5376]{1,0:T(8,128)} %param.17), kind=kLoop, calls=%fused_computation.16 | loop fusion | flops 23396352 | bytes 41287684 | tf_op jit(solution)/shard_map/convert_element_type | solution.py:328
  308.5 0.0 copy-start
  308.5 0.0 copy-start.1
  308.5 0.0 copy-start.2
  308.5 7.2 %fusion.5 = (bf16[128,5376]{1,0:T(8,128)(2,1)}, f32[128,5376]{1,0:T(8,128)}, f32[128,5376]{1,0:T(8,128)}, f32[128,5376]{1,0:T(8,128)}) fusion(f32[128,5376]{1,0:T(8,128)} %param.18, f32[128,5376]{1,0:T(8,128)S(1)} %get-tuple-element.18, f32[]{:T(128)} %bitcast.2, f32[128,5376]{1,0:T(8,128)} %param.19, f32[128,5376]{1,0:T(8,128)} %param.20), kind=kLoop, calls=%fused_computation.15 | loop fusion | flops 11698176 | bytes 20643844 | tf_op jit(solution)/shard_map/convert_element_type | solution.py:328
  315.7 0.0 copy-done
  315.7 0.0 copy-done.1
  315.7 0.0 copy-done.2
  315.7 1.3 fusion.3
  (2 shorter events, 0.0 us)
Async XLA Ops:
  1.6 295.6 %slice-start = ((s8[5505024]{0:T(1024)(128)(4,1)}), s8[4194304]{0:T(1024)(128)(4,1)S(1)}, s32[]{:S(2)}) async-start(s8[5505024]{0:T(1024)(128)(4,1)} %bitcast.9), calls=%async_computation | async-start | bytes 8388608
  1.6 295.6 %slice-start.2 = ((s8[5505024]{0:T(1024)(128)(4,1)}), s8[4194304]{0:T(1024)(128)(4,1)S(1)}, s32[]{:S(2)}) async-start(s8[5505024]{0:T(1024)(128)(4,1)} %bitcast.11), calls=%async_computation.2 | async-start | bytes 8388608
  1.6 295.6 %slice-start.1 = ((s8[5505024]{0:T(1024)(128)(4,1)}), s8[1310720]{0:T(1024)(128)(4,1)S(1)}, s32[]{:S(2)}) async-start(s8[5505024]{0:T(1024)(128)(4,1)} %bitcast.9), calls=%async_computation.1 | async-start | bytes 2621440
  1.6 295.6 %slice-start.3 = ((s8[5505024]{0:T(1024)(128)(4,1)}), s8[1310720]{0:T(1024)(128)(4,1)S(1)}, s32[]{:S(2)}) async-start(s8[5505024]{0:T(1024)(128)(4,1)} %bitcast.11), calls=%async_computation.3 | async-start | bytes 2621440
  308.5 7.2 %copy-start = (f32[9,672]{1,0:T(8,128)S(1)}, f32[9,672]{1,0:T(8,128)}, u32[]{:S(2)}) copy-start(f32[9,672]{1,0:T(8,128)} %param.21) | copy-start | bytes 72580
  308.5 7.2 %copy-start.1 = (f32[9,672]{1,0:T(8,128)S(1)}, f32[9,672]{1,0:T(8,128)}, u32[]{:S(2)}) copy-start(f32[9,672]{1,0:T(8,128)} %param.22) | copy-start | bytes 72580
  308.5 7.2 %copy-start.2 = (f32[9,672]{1,0:T(8,128)S(1)}, f32[9,672]{1,0:T(8,128)}, u32[]{:S(2)}) copy-start(f32[9,672]{1,0:T(8,128)} %param.23) | copy-start | bytes 72580

commit v2 on v1

v2 whole, which is shorter than its diff:
```python
import functools

import jax
import jax.numpy as jnp
from jax import lax
from jax.experimental import pallas as pl
from jax.experimental.pallas import tpu as pltpu
from jax.sharding import PartitionSpec as P

LEARN_RATE = 0.003
BETA_ONE = 0.9
BETA_TWO = 0.95
ADAM_EPS = 1e-8
WEIGHT_DECAY = 0.1
CLIP_NORM = 1.0
ADAM_STEP = 10

MESH = pl.DeviceIdType.MESH
F32 = jnp.float32

WIDTH = 5376
NORM_ROWS = 9
NORM_COLS = 672
NORM_PAD = (16, 768)
ROWS = 8
A_COLS = 2176
B_COLS = 2176
HALF = 256
B_AT = A_COLS
C_AT = A_COLS + B_COLS
D_AT = C_AT + 2 * HALF
LAG_ZERO = 3
LAG = 2
P_SLOTS = 8
R_SLOTS = 6
SEND_SLOTS = 8
RING = 16


def reduce_kernel(counts, emb, mat, norm, emb_out, mat_out, norm_out, scale_out,
                  part, recv_zero, xa, yb, zc, zd, ya, xb, xc, yd, yc, xd, grad, square,
                  norm_in, norm_part, norm_a, norm_b, norm_c, norm_d, sum_send, sum_recv, scale,
                  load_sem, zero_send, zero_recv, credit,
                  one_send, one_recv, two_send, two_recv, three_send, three_recv, four_send, four_recv, out_sem,
                  norm_load, norm_send, norm_recv, norm_store, sum_ssem, sum_rsem, scale_sem):
    emb_count, mat_count = counts
    total = emb_count + mat_count
    z = lax.axis_index("dp")
    f = lax.axis_index("fsdp")
    c = lax.rem(f, 2)
    x = lax.rem(lax.div(f, 2), 2)
    y = lax.div(f, 4)
    core = (z, f + 1 - 2 * c)
    xn = (z, f + 2 - 4 * x)
    yn = (z, f + 4 - 8 * y)
    zn = (1 - z, f)
    peers = [(z, lax.rem(f + k, 8)) for k in range(1, 8)]

    def remote(src, dst, ssem, rsem, dev):
        return pltpu.make_async_remote_copy(src_ref=src, dst_ref=dst, send_sem=ssem, recv_sem=rsem,
                                            device_id=dev, device_id_type=MESH)

    def half_at(base, which):
        return pl.ds(pl.multiple_of(base + which * HALF, 128), HALF)

    c_keep, c_give = half_at(C_AT, z), half_at(C_AT, 1 - z)
    d_keep, d_give = half_at(D_AT, z), half_at(D_AT, 1 - z)
    a_cols, b_cols = pl.ds(0, A_COLS), pl.ds(B_AT, B_COLS)

    barrier = pltpu.get_barrier_semaphore()
    for dev in peers + [zn]:
        pl.semaphore_signal(barrier, inc=1, device_id=dev, device_id_type=MESH)
    norm_copy = pltpu.make_async_copy(norm, norm_in, norm_load)
    norm_copy.start()

    def on_rows(j, body):
        @pl.when(j < emb_count)
        def _():
            body(emb, emb_out, pl.multiple_of(j * ROWS, ROWS))

        @pl.when(j >= emb_count)
        def _():
            body(mat, mat_out, pl.multiple_of((j - emb_count) * ROWS, ROWS))

    def load_copy(ref, row, j):
        s = lax.rem(j, P_SLOTS)
        return pltpu.make_async_copy(ref.at[:, :, c, pl.ds(row, ROWS), :], part.at[s], load_sem.at[s])

    def zero_copy(ref, row, j):
        s = lax.rem(j, R_SLOTS)
        return remote(ref.at[:, :, 1 - c, pl.ds(row, ROWS), :], recv_zero.at[s], zero_send.at[s], zero_recv.at[s], core)

    def ones(j):
        s, r = lax.rem(j, P_SLOTS), lax.rem(j, RING)
        return (remote(part.at[s, :, :, :, c_give], zc.at[r], one_send.at[2, s], one_recv.at[2, r], zn),
                remote(part.at[s, :, :, :, d_give], zd.at[r], one_send.at[3, s], one_recv.at[3, r], zn),
                remote(part.at[s, :, 1 - x, :, a_cols], xa.at[r], one_send.at[0, s], one_recv.at[0, r], xn),
                remote(part.at[s, 1 - y, :, :, b_cols], yb.at[r], one_send.at[1, s], one_recv.at[1, r], yn))

    def twos(j):
        s, r = lax.rem(j, SEND_SLOTS), lax.rem(j, RING)
        return (remote(zc.at[r, :, 1 - x], xc.at[r], two_send.at[2, s], two_recv.at[2, r], xn),
                remote(zd.at[r, 1 - y], yd.at[r], two_send.at[3, s], two_recv.at[3, r], yn),
                remote(xa.at[r, 1 - y], ya.at[r], two_send.at[0, s], two_recv.at[0, r], yn),
                remote(yb.at[r, 1 - x], xb.at[r], two_send.at[1, s], two_recv.at[1, r], xn))

    def threes(j):
        s, r = lax.rem(j, SEND_SLOTS), lax.rem(j, RING)
        return (remote(xc.at[r, 1 - y], yc.at[r], three_send.at[2, s], three_recv.at[2, r], yn),
                remote(yd.at[r, 1 - x], xd.at[r], three_send.at[3, s], three_recv.at[3, r], xn),
                remote(ya.at[r], grad.at[r, :, a_cols], three_send.at[0, s], three_recv.at[0, r], zn),
                remote(xb.at[r], grad.at[r, :, b_cols], three_send.at[1, s], three_recv.at[1, r], zn))

    def fours(j, c_at, d_at):
        s, r = lax.rem(j, SEND_SLOTS), lax.rem(j, RING)
        return (remote(grad.at[r, :, c_at], grad.at[r, :, c_at], four_send.at[0, s], four_recv.at[0, r], zn),
                remote(grad.at[r, :, d_at], grad.at[r, :, d_at], four_send.at[1, s], four_recv.at[1, r], zn))

    def out_copy(ref, row, j):
        return pltpu.make_async_copy(grad.at[lax.rem(j, RING)], ref.at[pl.ds(row, ROWS), :],
                                     out_sem.at[lax.rem(j, SEND_SLOTS)])

    norm_zero = remote(norm_part.at[:, :, 1 - c], norm_a, norm_send.at[0], norm_recv.at[0], core)
    norm_one = remote(norm_a.at[:, 1 - x], norm_b, norm_send.at[1], norm_recv.at[1], xn)
    norm_two = remote(norm_b.at[1 - y], norm_c, norm_send.at[2], norm_recv.at[2], yn)
    norm_three = remote(norm_c, norm_d, norm_send.at[3], norm_recv.at[3], zn)

    def when_in(j, body):
        pl.when(jnp.logical_and(j >= 0, j < total))(functools.partial(body, j))

    def start(copies):
        for copy in copies:
            copy.start()

    def wait_send(copies):
        for copy in copies:
            copy.wait_send()

    def stage_issue(j):
        @pl.when(j >= P_SLOTS)
        def _():
            wait_send(ones(j - P_SLOTS))

        @pl.when(j >= R_SLOTS)
        def _():
            zero_copy(emb, 0, j - R_SLOTS).wait_send()
            pl.semaphore_wait(credit, 1)

        def body(ref, _, row):
            zero_copy(ref, row, j).start()
            load_copy(ref, row, j).start()

        on_rows(j, body)

    def stage_one(j):
        load_copy(emb, 0, j).wait()
        zero_copy(emb, 0, j).wait_recv()
        part[lax.rem(j, P_SLOTS)] += recv_zero[lax.rem(j, R_SLOTS)]

        @pl.when(j + R_SLOTS < total)
        def _():
            pl.semaphore_signal(credit, inc=1, device_id=core, device_id_type=MESH)

        start(ones(j))

    def stage_two(j):
        s, r = lax.rem(j, P_SLOTS), lax.rem(j, RING)
        for copy in ones(j):
            copy.wait_recv()
        zc[r] += part[s, :, :, :, c_keep]
        zd[r] += part[s, :, :, :, d_keep]
        xa[r] += part[s, :, x, :, a_cols]
        yb[r] += part[s, y, :, :, b_cols]

        @pl.when(j >= SEND_SLOTS)
        def _():
            wait_send(twos(j - SEND_SLOTS))

        start(twos(j))

    def stage_three(j):
        r = lax.rem(j, RING)
        for copy in twos(j):
            copy.wait_recv()
        xc[r] += zc[r, :, x]
        yd[r] += zd[r, y]
        ya[r] += xa[r, y]
        xb[r] += yb[r, x]

        @pl.when(j >= SEND_SLOTS)
        def _():
            wait_send(threes(j - SEND_SLOTS))

        start(threes(j))

    def stage_four(j):
        r = lax.rem(j, RING)
        for copy in threes(j):
            copy.wait_recv()

        @pl.when(j >= SEND_SLOTS)
        def _():
            wait_send(fours(j - SEND_SLOTS, c_keep, d_keep))

        grad[r, :, c_keep] = (yc[r] + xc[r, y]) * (1.0 / 16.0)
        grad[r, :, d_keep] = (xd[r] + yd[r, x]) * (1.0 / 16.0)
        left = (grad[r, :, a_cols] + ya[r]) * (1.0 / 16.0)
        right = (grad[r, :, b_cols] + xb[r]) * (1.0 / 16.0)
        grad[r, :, a_cols] = left
        grad[r, :, b_cols] = right
        square[:, a_cols] += left * left
        square[:, b_cols] += right * right
        start(fours(j, c_keep, d_keep))

    def stage_five(j):
        r = lax.rem(j, RING)
        for copy in fours(j, c_give, d_give):
            copy.wait_recv()
        rest = grad[r, :, C_AT:]
        square[:, C_AT:] += rest * rest

        @pl.when(j >= SEND_SLOTS)
        def _():
            out_copy(emb_out, 0, j - SEND_SLOTS).wait()

        def body(_, ref, row):
            out_copy(ref, row, j).start()

        on_rows(j, body)

    def trip(it, carry):
        when_in(it, stage_issue)
        when_in(it - LAG_ZERO, stage_one)
        when_in(it - LAG_ZERO - LAG, stage_two)
        when_in(it - LAG_ZERO - 2 * LAG, stage_three)
        when_in(it - LAG_ZERO - 3 * LAG, stage_four)
        when_in(it - LAG_ZERO - 4 * LAG, stage_five)

        @pl.when(it == 5)
        def _():
            norm_copy.wait()
            for k in range(8):
                norm_part[k // 4, (k // 2) % 2, k % 2, :NORM_ROWS, :NORM_COLS] = norm_in[:, k * NORM_COLS:(k + 1) * NORM_COLS]
            norm_zero.start()

        @pl.when(it == 8)
        def _():
            norm_zero.wait_recv()
            norm_a[...] += norm_part[:, :, c]
            norm_one.start()

        @pl.when(it == 12)
        def _():
            norm_one.wait_recv()
            norm_b[...] += norm_a[:, x]
            norm_two.start()

        @pl.when(it == 16)
        def _():
            norm_two.wait_recv()
            norm_c[...] += norm_b[y]
            norm_three.start()

        @pl.when(it == 20)
        def _():
            norm_three.wait_recv()
            norm_d[...] = (norm_d[...] + norm_c[...]) * (1.0 / 16.0)
            pltpu.make_async_copy(norm_d, norm_out, norm_store).start()

        return carry

    pl.semaphore_wait(barrier, 8)
    norm_part[...] = jnp.zeros_like(norm_part)
    square[...] = jnp.zeros_like(square)
    lax.fori_loop(0, total + LAG_ZERO + 4 * LAG, trip, 0)

    norm_sq = norm_d[...] * norm_d[...]
    local = jnp.sum(square[...]) + jnp.sum(norm_sq)
    value = jnp.full((8, 128), local, F32)
    sum_send[...] = value
    sum_recv[f] = value
    sums = [remote(sum_send, sum_recv.at[f], sum_ssem.at[k], sum_rsem.at[f], dev) for k, dev in enumerate(peers)]
    start(sums)
    for k in range(1, 8):
        s = lax.rem(f + k, 8)
        remote(sum_send, sum_recv.at[s], sum_ssem.at[0], sum_rsem.at[s], core).wait_recv()
    whole = sum_recv[0]
    for k in range(1, 8):
        whole = whole + sum_recv[k]
    scale[...] = jnp.minimum(1.0, CLIP_NORM / jnp.sqrt(whole))
    scale_copy = pltpu.make_async_copy(scale, scale_out, scale_sem)
    scale_copy.start()

    wait_send(sums)
    wait_send((norm_zero, norm_one, norm_two, norm_three))
    pltpu.make_async_copy(norm_d, norm_out, norm_store).wait()

    def drain(slots, copies):
        def body(j, carry):
            wait_send(copies(j))
            return carry
        lax.fori_loop(total - slots, total, body, 0)

    drain(P_SLOTS, ones)
    drain(R_SLOTS, lambda j: (zero_copy(emb, 0, j),))
    drain(SEND_SLOTS, lambda j: twos(j) + threes(j) + fours(j, c_keep, d_keep))

    def last(j, carry):
        out_copy(emb_out, 0, j).wait()
        return carry

    lax.fori_loop(total - SEND_SLOTS, total, last, 0)
    scale_copy.wait()


def reduce_grads(emb_grad, mat_grad, norm_grad):
    emb_rows = emb_grad.shape[0] // 8
    mat_rows = mat_grad.shape[0] // 8
    counts = (emb_rows // ROWS, mat_rows // ROWS)
    dma = pltpu.SemaphoreType.DMA
    scratch = [
        pltpu.VMEM((P_SLOTS, 2, 2, ROWS, WIDTH), F32),
        pltpu.VMEM((R_SLOTS, 2, 2, ROWS, WIDTH), F32),
        pltpu.VMEM((RING, 2, ROWS, A_COLS), F32),
        pltpu.VMEM((RING, 2, ROWS, B_COLS), F32),
        pltpu.VMEM((RING, 2, 2, ROWS, HALF), F32),
        pltpu.VMEM((RING, 2, 2, ROWS, HALF), F32),
        pltpu.VMEM((RING, ROWS, A_COLS), F32),
        pltpu.VMEM((RING, ROWS, B_COLS), F32),
        pltpu.VMEM((RING, 2, ROWS, HALF), F32),
        pltpu.VMEM((RING, 2, ROWS, HALF), F32),
        pltpu.VMEM((RING, ROWS, HALF), F32),
        pltpu.VMEM((RING, ROWS, HALF), F32),
        pltpu.VMEM((RING, ROWS, WIDTH), F32),
        pltpu.VMEM((ROWS, WIDTH), F32),
        pltpu.VMEM((NORM_ROWS, WIDTH), F32),
        pltpu.VMEM((2, 2, 2) + NORM_PAD, F32),
        pltpu.VMEM((2, 2) + NORM_PAD, F32),
        pltpu.VMEM((2,) + NORM_PAD, F32),
        pltpu.VMEM(NORM_PAD, F32),
        pltpu.VMEM(NORM_PAD, F32),
        pltpu.VMEM((8, 128), F32),
        pltpu.VMEM((8, 8, 128), F32),
        pltpu.VMEM((8, 128), F32),
        dma((P_SLOTS,)), dma((R_SLOTS,)), dma((R_SLOTS,)), pltpu.SemaphoreType.REGULAR,
        dma((4, P_SLOTS)), dma((4, RING)), dma((4, SEND_SLOTS)), dma((4, RING)),
        dma((4, SEND_SLOTS)), dma((4, RING)), dma((2, SEND_SLOTS)), dma((2, RING)), dma((SEND_SLOTS,)),
        dma, dma((4,)), dma((4,)), dma, dma((7,)), dma((8,)), dma,
    ]
    hbm = pl.BlockSpec(memory_space=pl.ANY)
    return pl.pallas_call(
        functools.partial(reduce_kernel, counts),
        out_shape=(
            jax.ShapeDtypeStruct((emb_rows, WIDTH), F32),
            jax.ShapeDtypeStruct((mat_rows, WIDTH), F32),
            jax.ShapeDtypeStruct(NORM_PAD, F32),
            jax.ShapeDtypeStruct((8, 128), F32),
        ),
        in_specs=[hbm] * 3,
        out_specs=(hbm,) * 4,
        scratch_shapes=scratch,
        compiler_params=pltpu.CompilerParams(
            collective_id=0, has_side_effects=True, vmem_limit_bytes=25 * 1024 * 1024
        ),
        name="reduce_grads",
    )(emb_grad.reshape(2, 2, 2, emb_rows, WIDTH), mat_grad.reshape(2, 2, 2, mat_rows, WIDTH), norm_grad)


def adamw_update(grad_part, param_old, mom_old, var_old, decay_rate):
    new_mom = BETA_ONE * mom_old + (1.0 - BETA_ONE) * grad_part
    new_var = BETA_TWO * var_old + (1.0 - BETA_TWO) * grad_part * grad_part
    mom_hat = new_mom / (1.0 - BETA_ONE ** ADAM_STEP)
    var_hat = new_var / (1.0 - BETA_TWO ** ADAM_STEP)
    step_dir = mom_hat / (jnp.sqrt(var_hat) + ADAM_EPS)
    new_param = param_old - LEARN_RATE * (step_dir + decay_rate * param_old)
    return (new_param, new_mom, new_var, new_param.astype(jnp.bfloat16))


def solution(mesh):
    def local_step(emb_grad, mat_grad, norm_grad, emb_param, emb_mom, emb_var, mat_param, mat_mom, mat_var, norm_param, norm_mom, norm_var):
        emb_mean, mat_mean, norm_mean, scale = reduce_grads(emb_grad[0, 0], mat_grad[0, 0], norm_grad[0, 0])
        clip_scale = scale[0, 0]
        emb_out = adamw_update(emb_mean * clip_scale, emb_param, emb_mom, emb_var, WEIGHT_DECAY)
        mat_out = adamw_update(mat_mean * clip_scale, mat_param, mat_mom, mat_var, WEIGHT_DECAY)
        norm_out = adamw_update(norm_mean[:NORM_ROWS, :NORM_COLS] * clip_scale, norm_param, norm_mom, norm_var, 0.0)
        return emb_out + mat_out + norm_out

    grad_spec = P("dp", "fsdp", None, None)
    row_spec = P("fsdp", None)
    col_spec = P(None, "fsdp")
    in_list = (grad_spec, grad_spec, grad_spec, row_spec, row_spec, row_spec, row_spec, row_spec, row_spec, col_spec, col_spec, col_spec)
    out_list = (row_spec, row_spec, row_spec, row_spec, row_spec, row_spec, row_spec, row_spec, col_spec, col_spec, col_spec, col_spec)
    return jax.shard_map(local_step, mesh=mesh, in_specs=in_list, out_specs=out_list, check_vma=False)
```

time: 317 us -> 290 us (0.915)
  Pallas kernels: 295 us -> 268 us
    pallas_call x1, Pallas kernels: 295 us -> 268 us  [reduce_grads(): pl.pallas_call(functools.partial(reduce_kernel, counts), out_shape=(jax.S...]
where the time goes in v2:
time: 290 us
  Pallas kernels  268 us (92%)
  other arithmetic  19.8 us (7%)
    pallas_call x1, Pallas kernels, reduce_grads(): pl.pallas_call(functools.partial(reduce_kernel, counts), out_shape=(jax.S...  268 us
    convert_element_type x3, other arithmetic, adamw_update(): return (new_param, new_mom, new_var, new_param.astype(jnp.bfloat16))  19.8 us

profile of v2, /device:TPU:0, one launch (start us, length us, event | category | flops | bytes accessed | tf_op | source)
XLA Modules:
  0.0 289.7 jit_solution(13223810948516560216)
XLA Ops:
  0.6 1.0 copy.26
  1.6 0.0 slice-start
  1.6 0.0 slice-start.1
  1.6 267.7 %reduce_grads.1 = (f32[256,5376]{1,0:T(8,128)S(1)}, f32[128,5376]{1,0:T(8,128)S(1)}, f32[16,768]{1,0:T(8,128)S(1)}, f32[8,128]{1,0:T(8,128)S(1)}) custom-call(f32[2,2,2,256,5376]{4,3,2,1,0:T(8,128)} %bitcast.7, f32[2,2,2,128,5376]{4,3,2,1,0:T(8,128)} %bitcast.8, f32[9,5376]{1,0:T(8,128)S(1)} %bitcast.6), custom_call_target="tpu_custom_call" | custom-call | tf_op jit(solution)/shard_map/reduce_grads/pallas_call | solution.py:351
  269.4 0.5 slice.6
  269.9 0.0 slice-done
  269.9 0.0 slice-done.1
  269.9 11.3 %fusion.7 = (bf16[256,5376]{1,0:T(8,128)(2,1)}, f32[256,5376]{1,0:T(8,128)}, f32[256,5376]{1,0:T(8,128)}, f32[256,5376]{1,0:T(8,128)}) fusion(f32[256,5376]{1,0:T(8,128)S(1)} %bitcast.10, f32[256,5376]{1,0:T(8,128)S(1)} %get-tuple-element.16, f32[]{:T(128)} %bitcast.2, f32[256,5376]{1,0:T(8,128)} %param.16, f32[256,5376]{1,0:T(8,128)} %param.17), kind=kLoop, calls=%fused_computation.16 | loop fusion | flops 23396352 | bytes 41287684 | tf_op jit(solution)/shard_map/convert_element_type | solution.py:376
  281.2 0.0 copy-start
  281.2 0.0 copy-start.1
  281.2 0.0 copy-start.2
  281.2 7.2 %fusion.5 = (bf16[128,5376]{1,0:T(8,128)(2,1)}, f32[128,5376]{1,0:T(8,128)}, f32[128,5376]{1,0:T(8,128)}, f32[128,5376]{1,0:T(8,128)}) fusion(f32[128,5376]{1,0:T(8,128)} %param.18, f32[128,5376]{1,0:T(8,128)S(1)} %get-tuple-element.18, f32[]{:T(128)} %bitcast.2, f32[128,5376]{1,0:T(8,128)} %param.19, f32[128,5376]{1,0:T(8,128)} %param.20), kind=kLoop, calls=%fused_computation.15 | loop fusion | flops 11698176 | bytes 20643844 | tf_op jit(solution)/shard_map/convert_element_type | solution.py:376
  288.4 0.0 copy-done
  288.4 0.0 copy-done.1
  288.4 0.0 copy-done.2
  288.4 1.3 fusion.3
  (1 shorter events, 0.0 us)
Async XLA Ops:
  1.6 268.3 %slice-start = ((s8[5505024]{0:T(1024)(128)(4,1)}), s8[4194304]{0:T(1024)(128)(4,1)S(1)}, s32[]{:S(2)}) async-start(s8[5505024]{0:T(1024)(128)(4,1)} %bitcast.9), calls=%async_computation | async-start | bytes 8388608
  1.6 268.3 %slice-start.1 = ((s8[5505024]{0:T(1024)(128)(4,1)}), s8[1310720]{0:T(1024)(128)(4,1)S(1)}, s32[]{:S(2)}) async-start(s8[5505024]{0:T(1024)(128)(4,1)} %bitcast.9), calls=%async_computation.1 | async-start | bytes 2621440
  281.2 7.2 %copy-start = (f32[9,672]{1,0:T(8,128)S(1)}, f32[9,672]{1,0:T(8,128)}, u32[]{:S(2)}) copy-start(f32[9,672]{1,0:T(8,128)} %param.21) | copy-start | bytes 72580
  281.2 7.2 %copy-start.1 = (f32[9,672]{1,0:T(8,128)S(1)}, f32[9,672]{1,0:T(8,128)}, u32[]{:S(2)}) copy-start(f32[9,672]{1,0:T(8,128)} %param.22) | copy-start | bytes 72580
  281.2 7.2 %copy-start.2 = (f32[9,672]{1,0:T(8,128)S(1)}, f32[9,672]{1,0:T(8,128)}, u32[]{:S(2)}) copy-start(f32[9,672]{1,0:T(8,128)} %param.23) | copy-start | bytes 72580

commit v3 on v2

--- a/solution.py
+++ b/solution.py
@@ -1,4 +1,5 @@
 import functools
+import math
 
 import jax
 import jax.numpy as jnp
@@ -240,7 +241,8 @@
         def _():
             norm_copy.wait()
             for k in range(8):
-                norm_part[k // 4, (k // 2) % 2, k % 2, :NORM_ROWS, :NORM_COLS] = norm_in[:, k * NORM_COLS:(k + 1) * NORM_COLS]
+                for row in range(NORM_ROWS):
+                    norm_part[k // 4, (k // 2) % 2, k % 2, row:row + 1, :NORM_COLS] = norm_in[row, :, k * NORM_COLS:(k + 1) * NORM_COLS]
             norm_zero.start()
 
         @pl.when(it == 8)
@@ -333,7 +335,7 @@
         pltpu.VMEM((RING, ROWS, HALF), F32),
         pltpu.VMEM((RING, ROWS, WIDTH), F32),
         pltpu.VMEM((ROWS, WIDTH), F32),
-        pltpu.VMEM((NORM_ROWS, WIDTH), F32),
+        pltpu.VMEM((NORM_ROWS, 1, WIDTH), F32),
         pltpu.VMEM((2, 2, 2) + NORM_PAD, F32),
         pltpu.VMEM((2, 2) + NORM_PAD, F32),
         pltpu.VMEM((2,) + NORM_PAD, F32),
@@ -356,34 +358,116 @@
             jax.ShapeDtypeStruct(NORM_PAD, F32),
             jax.ShapeDtypeStruct((8, 128), F32),
         ),
-        in_specs=[hbm] * 3,
+        in_specs=[pl.BlockSpec(memory_space=pltpu.HBM)] * 3,
         out_specs=(hbm,) * 4,
         scratch_shapes=scratch,
         compiler_params=pltpu.CompilerParams(
             collective_id=0, has_side_effects=True, vmem_limit_bytes=25 * 1024 * 1024
         ),
         name="reduce_grads",
-    )(emb_grad.reshape(2, 2, 2, emb_rows, WIDTH), mat_grad.reshape(2, 2, 2, mat_rows, WIDTH), norm_grad)
-
-
-def adamw_update(grad_part, param_old, mom_old, var_old, decay_rate):
-    new_mom = BETA_ONE * mom_old + (1.0 - BETA_ONE) * grad_part
-    new_var = BETA_TWO * var_old + (1.0 - BETA_TWO) * grad_part * grad_part
-    mom_hat = new_mom / (1.0 - BETA_ONE ** ADAM_STEP)
-    var_hat = new_var / (1.0 - BETA_TWO ** ADAM_STEP)
-    step_dir = mom_hat / (jnp.sqrt(var_hat) + ADAM_EPS)
-    new_param = param_old - LEARN_RATE * (step_dir + decay_rate * param_old)
-    return (new_param, new_mom, new_var, new_param.astype(jnp.bfloat16))
+    )(emb_grad.reshape(2, 2, 2, emb_rows, WIDTH), mat_grad.reshape(2, 2, 2, mat_rows, WIDTH),
+      norm_grad.reshape(NORM_ROWS, 1, WIDTH))
+
+
+BLOCK = 16
+COLS = 384
+STORE_SLOTS = 4
+
+
+def adamw_block(grad, param, mom, var, decay_rate):
+    new_mom = BETA_ONE * mom + (1.0 - BETA_ONE) * grad
+    new_var = BETA_TWO * var + (1.0 - BETA_TWO) * grad * grad
+    root = math.sqrt(1.0 - BETA_TWO ** ADAM_STEP)
+    step_dir = new_mom / (jnp.sqrt(new_var) + ADAM_EPS * root)
+    rate = LEARN_RATE * root / (1.0 - BETA_ONE ** ADAM_STEP)
+    return param - (rate * step_dir + (LEARN_RATE * decay_rate) * param), new_mom, new_var
+
+
+def adamw_kernel(scale, eg, ep, em, ev, mg, mp, mm, mv, ng, np_, nm, nv,
+                 ep_out, em_out, ev_out, eb_out, mp_out, mm_out, mv_out, mb_out, np_out, nm_out, nv_out, nb_out,
+                 p_buf, m_buf, v_buf, b_buf, n_bufs, nb_buf, sems, n_sems):
+    clip = scale[0:1, 0:1]
+
+    def copies(outs, slot, row):
+        return [pltpu.make_async_copy(buf.at[slot], out.at[pl.ds(row, BLOCK), :], sems.at[k, slot])
+                for k, (buf, out) in enumerate(zip((p_buf, m_buf, v_buf, b_buf), outs))]
+
+    emb_outs = (ep_out, em_out, ev_out, eb_out)
+    mat_outs = (mp_out, mm_out, mv_out, mb_out)
+    emb_blocks = eg.shape[0] // BLOCK
+    mat_blocks = mg.shape[0] // BLOCK
+
+    def run(first, count, ins, outs):
+        def body(i, carry):
+            j = first + i
+            slot = lax.rem(j, STORE_SLOTS)
+
+            @pl.when(j >= STORE_SLOTS)
+            def _():
+                for copy in copies(emb_outs, slot, 0):
+                    copy.wait()
+
+            row = pl.multiple_of(i * BLOCK, BLOCK)
+            for col in range(0, WIDTH, COLS):
+                cols = pl.ds(col, COLS)
+                g, p, m, v = (ref[pl.ds(row, BLOCK), cols] for ref in ins)
+                new_p, new_m, new_v = adamw_block(g * clip, p, m, v, WEIGHT_DECAY)
+                p_buf[slot, :, cols] = new_p
+                m_buf[slot, :, cols] = new_m
+                v_buf[slot, :, cols] = new_v
+                b_buf[slot, :, cols] = new_p.astype(jnp.bfloat16)
+            for copy in copies(outs, slot, row):
+                copy.start()
+            return carry
+
+        lax.fori_loop(0, count, body, 0)
+
+    run(0, emb_blocks, (eg, ep, em, ev), emb_outs)
+    run(emb_blocks, mat_blocks, (mg, mp, mm, mv), mat_outs)
+    new_p, new_m, new_v = adamw_block(ng[:NORM_ROWS, :NORM_COLS] * clip, np_[...], nm[...], nv[...], 0.0)
+    for k, value in enumerate((new_p, new_m, new_v)):
+        n_bufs[k] = value
+    nb_buf[...] = new_p.astype(jnp.bfloat16)
+    norm_copies = [pltpu.make_async_copy(n_bufs.at[k], out, n_sems.at[k]) for k, out in enumerate((np_out, nm_out, nv_out))]
+    norm_copies.append(pltpu.make_async_copy(nb_buf, nb_out, n_sems.at[3]))
+    for copy in norm_copies:
+        copy.start()
+    for slot in range(STORE_SLOTS):
+        for copy in copies(emb_outs, slot, 0):
+            copy.wait()
+    for copy in norm_copies:
+        copy.wait()
+
+
+def adamw(scale, emb, mat, norm):
+    shapes = []
+    for ref in (emb[1], mat[1], norm[1]):
+        shapes += [jax.ShapeDtypeStruct(ref.shape, F32)] * 3 + [jax.ShapeDtypeStruct(ref.shape, jnp.bfloat16)]
+    buf = (STORE_SLOTS, BLOCK, WIDTH)
+    vmem = pl.BlockSpec(memory_space=pltpu.VMEM)
+    hbm = pl.BlockSpec(memory_space=pl.ANY)
+    elements = emb[1].size + mat[1].size
+    return pl.pallas_call(
+        adamw_kernel,
+        out_shape=tuple(shapes),
+        in_specs=[vmem] * 13,
+        out_specs=(hbm,) * 12,
+        scratch_shapes=[
+            pltpu.VMEM(buf, F32), pltpu.VMEM(buf, F32), pltpu.VMEM(buf, F32), pltpu.VMEM(buf, jnp.bfloat16),
+            pltpu.VMEM((3, NORM_ROWS, NORM_COLS), F32), pltpu.VMEM((NORM_ROWS, NORM_COLS), jnp.bfloat16),
+            pltpu.SemaphoreType.DMA((4, STORE_SLOTS)), pltpu.SemaphoreType.DMA((4,)),
+        ],
+        compiler_params=pltpu.CompilerParams(vmem_limit_bytes=8 * 1024 * 1024),
+        cost_estimate=pl.CostEstimate(flops=20 * elements, bytes_accessed=30 * elements, transcendentals=2 * elements),
+        name="adamw",
+    )(scale, *emb, *mat, *norm)
 
 
 def solution(mesh):
     def local_step(emb_grad, mat_grad, norm_grad, emb_param, emb_mom, emb_var, mat_param, mat_mom, mat_var, norm_param, norm_mom, norm_var):
         emb_mean, mat_mean, norm_mean, scale = reduce_grads(emb_grad[0, 0], mat_grad[0, 0], norm_grad[0, 0])
-        clip_scale = scale[0, 0]
-        emb_out = adamw_update(emb_mean * clip_scale, emb_param, emb_mom, emb_var, WEIGHT_DECAY)
-        mat_out = adamw_update(mat_mean * clip_scale, mat_param, mat_mom, mat_var, WEIGHT_DECAY)
-        norm_out = adamw_update(norm_mean[:NORM_ROWS, :NORM_COLS] * clip_scale, norm_param, norm_mom, norm_var, 0.0)
-        return emb_out + mat_out + norm_out
+        return adamw(scale, (emb_mean, emb_param, emb_mom, emb_var), (mat_mean, mat_param, mat_mom, mat_var),
+                     (norm_mean, norm_param, norm_mom, norm_var))
 
     grad_spec = P("dp", "fsdp", None, None)
     row_spec = P("fsdp", None)

time: 290 us -> 279 us (0.962)
  other arithmetic: 19.8 us -> 0 us
  Pallas kernels: 268 us -> 278 us
    convert_element_type x3 -> x0, other arithmetic: 19.8 us -> none  [adamw_update(): return (new_param, new_mom, new_var, new_param.astype(jnp.bfloat16))]
    pallas_call x0 -> x1, Pallas kernels: none -> 9.94 us  [adamw(): pl.pallas_call(adamw_kernel, out_shape=tuple(shapes), in_specs=[vmem] * 1...]
where the time goes in v3:
time: 279 us
  Pallas kernels  278 us (100%)
    pallas_call x1, Pallas kernels, reduce_grads(): pl.pallas_call(functools.partial(reduce_kernel, counts), out_shape=(jax.S...  268 us
    pallas_call x1, Pallas kernels, adamw(): pl.pallas_call(adamw_kernel, out_shape=tuple(shapes), in_specs=[vmem] * 1...  9.94 us

profile of v3, /device:TPU:0, one launch (start us, length us, event | category | flops | bytes accessed | tf_op | source)
XLA Modules:
  0.0 279.3 jit_solution(9603518437108386219)
XLA Ops:
  0.6 0.0 copy-start.6
  0.7 0.9 copy-done.6
  1.6 0.0 copy-start
  1.6 0.0 copy-start.1
  1.6 0.0 copy-start.2
  1.6 0.0 copy-start.3
  1.6 0.0 copy-start.4
  1.6 0.0 copy-start.5
  1.6 0.0 copy-start.7
  1.6 0.0 copy-start.8
  1.6 0.0 copy-start.9
  1.6 267.6 %reduce_grads.1 = (f32[256,5376]{1,0:T(8,128)S(1)}, f32[128,5376]{1,0:T(8,128)S(1)}, f32[16,768]{1,0:T(8,128)S(1)}, f32[8,128]{1,0:T(8,128)S(1)}) custom-call(f32[2,2,2,256,5376]{4,3,2,1,0:T(8,128)} %bitcast.4, f32[2,2,2,128,5376]{4,3,2,1,0:T(8,128)} %bitcast.5, f32[9,1,5376]{2,1,0:T(1,128)S(1)} %bitcast.3), custom_call_target="tpu_custom_call" | custom-call | tf_op jit(solution)/shard_map/reduce_grads/pallas_call | solution.py:353
  269.2 0.0 copy-done
  269.3 0.0 copy-done.1
  269.3 0.0 copy-done.2
  269.3 0.0 copy-done.3
  269.3 0.0 copy-done.4
  269.3 0.0 copy-done.5
  269.3 0.0 copy-done.7
  269.3 0.0 copy-done.8
  269.3 0.0 copy-done.9
  269.3 9.9 %adamw.1 = (f32[256,5376]{1,0:T(8,128)}, f32[256,5376]{1,0:T(8,128)}, f32[256,5376]{1,0:T(8,128)}, bf16[256,5376]{1,0:T(8,128)(2,1)}, f32[128,5376]{1,0:T(8,128)...) custom-call(f32[8,128]{1,0:T(8,128)S(1)} %get-tuple-element.16.scale, ...), custom_call_target="tpu_custom_call" | custom-call | flops 41287680 | bytes 61931520 | tf_op jit(solution)/shard_map/adamw/pallas_call | solution.py:450
Async XLA Ops:
  0.6 0.9 copy-start.6
  1.6 267.7 %copy-start = (f32[256,5376]{1,0:T(8,128)S(1)}, f32[256,5376]{1,0:T(8,128)}, u32[]{:S(2)}) copy-start(f32[256,5376]{1,0:T(8,128)} %ep.1) | copy-start | bytes 16515076
  1.6 267.7 %copy-start.1 = (f32[256,5376]{1,0:T(8,128)S(1)}, f32[256,5376]{1,0:T(8,128)}, u32[]{:S(2)}) copy-start(f32[256,5376]{1,0:T(8,128)} %em.1) | copy-start | bytes 16515076
  1.6 267.7 %copy-start.2 = (f32[256,5376]{1,0:T(8,128)S(1)}, f32[256,5376]{1,0:T(8,128)}, u32[]{:S(2)}) copy-start(f32[256,5376]{1,0:T(8,128)} %ev.1) | copy-start | bytes 16515076
  1.6 267.7 %copy-start.3 = (f32[128,5376]{1,0:T(8,128)S(1)}, f32[128,5376]{1,0:T(8,128)}, u32[]{:S(2)}) copy-start(f32[128,5376]{1,0:T(8,128)} %mp.1) | copy-start | bytes 8257540
  1.6 267.7 %copy-start.4 = (f32[128,5376]{1,0:T(8,128)S(1)}, f32[128,5376]{1,0:T(8,128)}, u32[]{:S(2)}) copy-start(f32[128,5376]{1,0:T(8,128)} %mm.1) | copy-start | bytes 8257540
  1.6 267.7 %copy-start.5 = (f32[128,5376]{1,0:T(8,128)S(1)}, f32[128,5376]{1,0:T(8,128)}, u32[]{:S(2)}) copy-start(f32[128,5376]{1,0:T(8,128)} %mv.1) | copy-start | bytes 8257540
  1.6 267.7 %copy-start.7 = (f32[9,672]{1,0:T(8,128)S(1)}, f32[9,672]{1,0:T(8,128)}, u32[]{:S(2)}) copy-start(f32[9,672]{1,0:T(8,128)} %np_.1) | copy-start | bytes 72580
  1.6 267.7 %copy-start.8 = (f32[9,672]{1,0:T(8,128)S(1)}, f32[9,672]{1,0:T(8,128)}, u32[]{:S(2)}) copy-start(f32[9,672]{1,0:T(8,128)} %nm.1) | copy-start | bytes 72580
  1.6 267.7 %copy-start.9 = (f32[9,672]{1,0:T(8,128)S(1)}, f32[9,672]{1,0:T(8,128)}, u32[]{:S(2)}) copy-start(f32[9,672]{1,0:T(8,128)} %nv.1) | copy-start | bytes 72580

commit v4 on v3

--- a/solution.py
+++ b/solution.py
@@ -24,12 +24,11 @@
 NORM_COLS = 672
 NORM_PAD = (16, 768)
 ROWS = 8
-A_COLS = 2176
-B_COLS = 2176
-HALF = 256
+A_COLS = 2048
+B_COLS = 2048
+HALF = 640
 B_AT = A_COLS
 C_AT = A_COLS + B_COLS
-D_AT = C_AT + 2 * HALF
 LAG_ZERO = 3
 LAG = 2
 P_SLOTS = 8
@@ -39,7 +38,7 @@
 
 
 def reduce_kernel(counts, emb, mat, norm, emb_out, mat_out, norm_out, scale_out,
-                  part, recv_zero, xa, yb, zc, zd, ya, xb, xc, yd, yc, xd, grad, square,
+                  part, recv_zero, xa, yb, zc, mid, wc, tc, grad, square,
                   norm_in, norm_part, norm_a, norm_b, norm_c, norm_d, sum_send, sum_recv, scale,
                   load_sem, zero_send, zero_recv, credit,
                   one_send, one_recv, two_send, two_recv, three_send, three_recv, four_send, four_recv, out_sem,
@@ -65,8 +64,7 @@
         return pl.ds(pl.multiple_of(base + which * HALF, 128), HALF)
 
     c_keep, c_give = half_at(C_AT, z), half_at(C_AT, 1 - z)
-    d_keep, d_give = half_at(D_AT, z), half_at(D_AT, 1 - z)
-    a_cols, b_cols = pl.ds(0, A_COLS), pl.ds(B_AT, B_COLS)
+    a_cols, b_cols, ab_cols = pl.ds(0, A_COLS), pl.ds(B_AT, B_COLS), pl.ds(0, C_AT)
 
     barrier = pltpu.get_barrier_semaphore()
     for dev in peers + [zn]:
@@ -94,28 +92,35 @@
     def ones(j):
         s, r = lax.rem(j, P_SLOTS), lax.rem(j, RING)
         return (remote(part.at[s, :, :, :, c_give], zc.at[r], one_send.at[2, s], one_recv.at[2, r], zn),
-                remote(part.at[s, :, :, :, d_give], zd.at[r], one_send.at[3, s], one_recv.at[3, r], zn),
                 remote(part.at[s, :, 1 - x, :, a_cols], xa.at[r], one_send.at[0, s], one_recv.at[0, r], xn),
                 remote(part.at[s, 1 - y, :, :, b_cols], yb.at[r], one_send.at[1, s], one_recv.at[1, r], yn))
 
+    def two_c_even(j):
+        s, r = lax.rem(j, SEND_SLOTS), lax.rem(j, RING)
+        return remote(zc.at[r, :, 1 - x], wc.at[r], two_send.at[2, s], two_recv.at[2, r], xn)
+
+    def two_c_odd(j):
+        s, r = lax.rem(j, SEND_SLOTS), lax.rem(j, RING)
+        return remote(zc.at[r, 1 - y], wc.at[r], two_send.at[2, s], two_recv.at[2, r], yn)
+
     def twos(j):
         s, r = lax.rem(j, SEND_SLOTS), lax.rem(j, RING)
-        return (remote(zc.at[r, :, 1 - x], xc.at[r], two_send.at[2, s], two_recv.at[2, r], xn),
-                remote(zd.at[r, 1 - y], yd.at[r], two_send.at[3, s], two_recv.at[3, r], yn),
-                remote(xa.at[r, 1 - y], ya.at[r], two_send.at[0, s], two_recv.at[0, r], yn),
-                remote(yb.at[r, 1 - x], xb.at[r], two_send.at[1, s], two_recv.at[1, r], xn))
-
-    def threes(j):
+        return (remote(xa.at[r, 1 - y], mid.at[r, :, a_cols], two_send.at[0, s], two_recv.at[0, r], yn),
+                remote(yb.at[r, 1 - x], mid.at[r, :, b_cols], two_send.at[1, s], two_recv.at[1, r], xn))
+
+    def three_c(j):
+        s, r, odd = lax.rem(j, SEND_SLOTS), lax.rem(j, RING), lax.rem(j, 2)
+        here = y + odd * (x - y)
+        step = (4 - 8 * y) + odd * ((2 - 4 * x) - (4 - 8 * y))
+        return remote(wc.at[r, 1 - here], tc.at[r], three_send.at[1, s], three_recv.at[1, r], (z, f + step))
+
+    def three_ab(j):
         s, r = lax.rem(j, SEND_SLOTS), lax.rem(j, RING)
-        return (remote(xc.at[r, 1 - y], yc.at[r], three_send.at[2, s], three_recv.at[2, r], yn),
-                remote(yd.at[r, 1 - x], xd.at[r], three_send.at[3, s], three_recv.at[3, r], xn),
-                remote(ya.at[r], grad.at[r, :, a_cols], three_send.at[0, s], three_recv.at[0, r], zn),
-                remote(xb.at[r], grad.at[r, :, b_cols], three_send.at[1, s], three_recv.at[1, r], zn))
-
-    def fours(j, c_at, d_at):
+        return remote(mid.at[r], grad.at[r, :, ab_cols], three_send.at[0, s], three_recv.at[0, r], zn)
+
+    def four(j, c_at):
         s, r = lax.rem(j, SEND_SLOTS), lax.rem(j, RING)
-        return (remote(grad.at[r, :, c_at], grad.at[r, :, c_at], four_send.at[0, s], four_recv.at[0, r], zn),
-                remote(grad.at[r, :, d_at], grad.at[r, :, d_at], four_send.at[1, s], four_recv.at[1, r], zn))
+        return remote(grad.at[r, :, c_at], grad.at[r, :, c_at], four_send.at[s], four_recv.at[r], zn)
 
     def out_copy(ref, row, j):
         return pltpu.make_async_copy(grad.at[lax.rem(j, RING)], ref.at[pl.ds(row, ROWS), :],
@@ -166,57 +171,63 @@
 
     def stage_two(j):
         s, r = lax.rem(j, P_SLOTS), lax.rem(j, RING)
+        even = lax.rem(j, 2) == 0
         for copy in ones(j):
             copy.wait_recv()
         zc[r] += part[s, :, :, :, c_keep]
-        zd[r] += part[s, :, :, :, d_keep]
         xa[r] += part[s, :, x, :, a_cols]
         yb[r] += part[s, y, :, :, b_cols]
 
         @pl.when(j >= SEND_SLOTS)
         def _():
-            wait_send(twos(j - SEND_SLOTS))
-
+            wait_send(twos(j - SEND_SLOTS) + (two_c_even(j - SEND_SLOTS),))
+
+        pl.when(even)(lambda: two_c_even(j).start())
+        pl.when(jnp.logical_not(even))(lambda: two_c_odd(j).start())
         start(twos(j))
 
     def stage_three(j):
         r = lax.rem(j, RING)
-        for copy in twos(j):
+        even = lax.rem(j, 2) == 0
+        for copy in twos(j) + (two_c_even(j),):
             copy.wait_recv()
-        xc[r] += zc[r, :, x]
-        yd[r] += zd[r, y]
-        ya[r] += xa[r, y]
-        xb[r] += yb[r, x]
+
+        @pl.when(even)
+        def _():
+            wc[r] += zc[r, :, x]
+
+        @pl.when(jnp.logical_not(even))
+        def _():
+            wc[r] += zc[r, y]
+
+        mid[r, :, a_cols] += xa[r, y]
+        mid[r, :, b_cols] += yb[r, x]
 
         @pl.when(j >= SEND_SLOTS)
         def _():
-            wait_send(threes(j - SEND_SLOTS))
-
-        start(threes(j))
+            wait_send((three_ab(j - SEND_SLOTS), three_c(j - SEND_SLOTS)))
+
+        start((three_c(j), three_ab(j)))
 
     def stage_four(j):
-        r = lax.rem(j, RING)
-        for copy in threes(j):
-            copy.wait_recv()
+        r, odd = lax.rem(j, RING), lax.rem(j, 2)
+        here = y + odd * (x - y)
+        three_c(j).wait_recv()
 
         @pl.when(j >= SEND_SLOTS)
         def _():
-            wait_send(fours(j - SEND_SLOTS, c_keep, d_keep))
-
-        grad[r, :, c_keep] = (yc[r] + xc[r, y]) * (1.0 / 16.0)
-        grad[r, :, d_keep] = (xd[r] + yd[r, x]) * (1.0 / 16.0)
-        left = (grad[r, :, a_cols] + ya[r]) * (1.0 / 16.0)
-        right = (grad[r, :, b_cols] + xb[r]) * (1.0 / 16.0)
-        grad[r, :, a_cols] = left
-        grad[r, :, b_cols] = right
-        square[:, a_cols] += left * left
-        square[:, b_cols] += right * right
-        start(fours(j, c_keep, d_keep))
+            four(j - SEND_SLOTS, c_keep).wait_send()
+
+        grad[r, :, c_keep] = (tc[r] + wc[r, here]) * (1.0 / 16.0)
+        three_ab(j).wait_recv()
+        both = (grad[r, :, ab_cols] + mid[r]) * (1.0 / 16.0)
+        grad[r, :, ab_cols] = both
+        square[:, ab_cols] += both * both
+        four(j, c_keep).start()
 
     def stage_five(j):
         r = lax.rem(j, RING)
-        for copy in fours(j, c_give, d_give):
-            copy.wait_recv()
+        four(j, c_give).wait_recv()
         rest = grad[r, :, C_AT:]
         square[:, C_AT:] += rest * rest
 
@@ -305,7 +316,7 @@
 
     drain(P_SLOTS, ones)
     drain(R_SLOTS, lambda j: (zero_copy(emb, 0, j),))
-    drain(SEND_SLOTS, lambda j: twos(j) + threes(j) + fours(j, c_keep, d_keep))
+    drain(SEND_SLOTS, lambda j: twos(j) + (two_c_even(j), three_ab(j), three_c(j), four(j, c_keep)))
 
     def last(j, carry):
         out_copy(emb_out, 0, j).wait()
@@ -326,12 +337,8 @@
         pltpu.VMEM((RING, 2, ROWS, A_COLS), F32),
         pltpu.VMEM((RING, 2, ROWS, B_COLS), F32),
         pltpu.VMEM((RING, 2, 2, ROWS, HALF), F32),
-        pltpu.VMEM((RING, 2, 2, ROWS, HALF), F32),
-        pltpu.VMEM((RING, ROWS, A_COLS), F32),
-        pltpu.VMEM((RING, ROWS, B_COLS), F32),
+        pltpu.VMEM((RING, ROWS, C_AT), F32),
         pltpu.VMEM((RING, 2, ROWS, HALF), F32),
-        pltpu.VMEM((RING, 2, ROWS, HALF), F32),
-        pltpu.VMEM((RING, ROWS, HALF), F32),
         pltpu.VMEM((RING, ROWS, HALF), F32),
         pltpu.VMEM((RING, ROWS, WIDTH), F32),
         pltpu.VMEM((ROWS, WIDTH), F32),
@@ -345,8 +352,8 @@
         pltpu.VMEM((8, 8, 128), F32),
         pltpu.VMEM((8, 128), F32),
         dma((P_SLOTS,)), dma((R_SLOTS,)), dma((R_SLOTS,)), pltpu.SemaphoreType.REGULAR,
-        dma((4, P_SLOTS)), dma((4, RING)), dma((4, SEND_SLOTS)), dma((4, RING)),
-        dma((4, SEND_SLOTS)), dma((4, RING)), dma((2, SEND_SLOTS)), dma((2, RING)), dma((SEND_SLOTS,)),
+        dma((3, P_SLOTS)), dma((3, RING)), dma((3, SEND_SLOTS)), dma((3, RING)),
+        dma((2, SEND_SLOTS)), dma((2, RING)), dma((SEND_SLOTS,)), dma((RING,)), dma((SEND_SLOTS,)),
         dma, dma((4,)), dma((4,)), dma, dma((7,)), dma((8,)), dma,
     ]
     hbm = pl.BlockSpec(memory_space=pl.ANY)
@@ -365,8 +372,9 @@
             collective_id=0, has_side_effects=True, vmem_limit_bytes=25 * 1024 * 1024
         ),
         name="reduce_grads",
-    )(emb_grad.reshape(2, 2, 2, emb_rows, WIDTH), mat_grad.reshape(2, 2, 2, mat_rows, WIDTH),
-      norm_grad.reshape(NORM_ROWS, 1, WIDTH))
+    )(*(pltpu.with_memory_space_constraint(grad, pltpu.HBM) for grad in (
+        emb_grad.reshape(2, 2, 2, emb_rows, WIDTH), mat_grad.reshape(2, 2, 2, mat_rows, WIDTH),
+        norm_grad.reshape(NORM_ROWS, 1, WIDTH))))
 
 
 BLOCK = 16

time: 279 us -> 274 us (0.982)
  Pallas kernels: 278 us -> 273 us
    pallas_call x1, Pallas kernels: 268 us -> 263 us  [reduce_grads(): pl.pallas_call(functools.partial(reduce_kernel, counts), out_shape=(jax.S...]
where the time goes in v4:
time: 274 us
  Pallas kernels  273 us (100%)
    pallas_call x1, Pallas kernels, reduce_grads(): pl.pallas_call(functools.partial(reduce_kernel, counts), out_shape=(jax.S...  263 us
    pallas_call x1, Pallas kernels, adamw(): pl.pallas_call(adamw_kernel, out_shape=tuple(shapes), in_specs=[vmem] * 1...  9.94 us

profile of v4, /device:TPU:0, one launch (start us, length us, event | category | flops | bytes accessed | tf_op | source)
XLA Modules:
  0.0 273.9 jit_solution(8354370075994171546)
XLA Ops:
  0.6 0.0 copy-start
  0.7 0.0 copy-start.1
  0.7 0.0 copy-start.2
  0.7 0.0 copy-start.3
  0.7 0.0 copy-start.4
  0.7 0.0 copy-start.5
  0.7 0.0 copy-start.6
  0.7 0.0 copy-start.7
  0.7 0.0 copy-start.8
  0.7 263.1 %reduce_grads.1 = (f32[256,5376]{1,0:T(8,128)S(1)}, f32[128,5376]{1,0:T(8,128)S(1)}, f32[16,768]{1,0:T(8,128)S(1)}, f32[8,128]{1,0:T(8,128)S(1)}) custom-call(f32[2,2,2,256,5376]{4,3,2,1,0:T(8,128)} %bitcast.3, f32[2,2,2,128,5376]{4,3,2,1,0:T(8,128)} %bitcast.4, f32[9,1,5376]{2,1,0:T(1,128)} %bitcast.5), custom_call_target="tpu_custom_call" | custom-call | tf_op jit(solution)/shard_map/reduce_grads/pallas_call | solution.py:360
  263.8 0.0 copy-done
  263.8 0.0 copy-done.1
  263.8 0.0 copy-done.2
  263.9 0.0 copy-done.3
  263.9 0.0 copy-done.4
  263.9 0.0 copy-done.5
  263.9 0.0 copy-done.6
  263.9 0.0 copy-done.7
  263.9 0.0 copy-done.8
  263.9 9.9 %adamw.1 = (f32[256,5376]{1,0:T(8,128)}, f32[256,5376]{1,0:T(8,128)}, f32[256,5376]{1,0:T(8,128)}, bf16[256,5376]{1,0:T(8,128)(2,1)}, f32[128,5376]{1,0:T(8,128)...) custom-call(f32[8,128]{1,0:T(8,128)S(1)} %get-tuple-element.16.scale, ...), custom_call_target="tpu_custom_call" | custom-call | flops 41287680 | bytes 61931520 | tf_op jit(solution)/shard_map/adamw/pallas_call | solution.py:458
Async XLA Ops:
  0.6 263.2 %copy-start = (f32[256,5376]{1,0:T(8,128)S(1)}, f32[256,5376]{1,0:T(8,128)}, u32[]{:S(2)}) copy-start(f32[256,5376]{1,0:T(8,128)} %ep.1) | copy-start | bytes 16515076
  0.7 263.2 %copy-start.1 = (f32[256,5376]{1,0:T(8,128)S(1)}, f32[256,5376]{1,0:T(8,128)}, u32[]{:S(2)}) copy-start(f32[256,5376]{1,0:T(8,128)} %em.1) | copy-start | bytes 16515076
  0.7 263.2 %copy-start.2 = (f32[256,5376]{1,0:T(8,128)S(1)}, f32[256,5376]{1,0:T(8,128)}, u32[]{:S(2)}) copy-start(f32[256,5376]{1,0:T(8,128)} %ev.1) | copy-start | bytes 16515076
  0.7 263.2 %copy-start.3 = (f32[128,5376]{1,0:T(8,128)S(1)}, f32[128,5376]{1,0:T(8,128)}, u32[]{:S(2)}) copy-start(f32[128,5376]{1,0:T(8,128)} %mp.1) | copy-start | bytes 8257540
  0.7 263.2 %copy-start.4 = (f32[128,5376]{1,0:T(8,128)S(1)}, f32[128,5376]{1,0:T(8,128)}, u32[]{:S(2)}) copy-start(f32[128,5376]{1,0:T(8,128)} %mm.1) | copy-start | bytes 8257540
  0.7 263.2 %copy-start.5 = (f32[128,5376]{1,0:T(8,128)S(1)}, f32[128,5376]{1,0:T(8,128)}, u32[]{:S(2)}) copy-start(f32[128,5376]{1,0:T(8,128)} %mv.1) | copy-start | bytes 8257540
  0.7 263.2 %copy-start.6 = (f32[9,672]{1,0:T(8,128)S(1)}, f32[9,672]{1,0:T(8,128)}, u32[]{:S(2)}) copy-start(f32[9,672]{1,0:T(8,128)} %np_.1) | copy-start | bytes 72580
  0.7 263.2 %copy-start.7 = (f32[9,672]{1,0:T(8,128)S(1)}, f32[9,672]{1,0:T(8,128)}, u32[]{:S(2)}) copy-start(f32[9,672]{1,0:T(8,128)} %nm.1) | copy-start | bytes 72580
  0.7 263.2 %copy-start.8 = (f32[9,672]{1,0:T(8,128)S(1)}, f32[9,672]{1,0:T(8,128)}, u32[]{:S(2)}) copy-start(f32[9,672]{1,0:T(8,128)} %nv.1) | copy-start | bytes 72580

commit v5 on v4

--- a/solution.py
+++ b/solution.py
@@ -30,11 +30,11 @@
 B_AT = A_COLS
 C_AT = A_COLS + B_COLS
 LAG_ZERO = 3
-LAG = 2
-P_SLOTS = 8
+LAG = 3
+P_SLOTS = 10
 R_SLOTS = 6
 SEND_SLOTS = 8
-RING = 16
+RING = 20
 
 
 def reduce_kernel(counts, emb, mat, norm, emb_out, mat_out, norm_out, scale_out,
@@ -219,14 +219,14 @@
             four(j - SEND_SLOTS, c_keep).wait_send()
 
         grad[r, :, c_keep] = (tc[r] + wc[r, here]) * (1.0 / 16.0)
+        four(j, c_keep).start()
+
+    def stage_five(j):
+        r = lax.rem(j, RING)
         three_ab(j).wait_recv()
         both = (grad[r, :, ab_cols] + mid[r]) * (1.0 / 16.0)
         grad[r, :, ab_cols] = both
         square[:, ab_cols] += both * both
-        four(j, c_keep).start()
-
-    def stage_five(j):
-        r = lax.rem(j, RING)
         four(j, c_give).wait_recv()
         rest = grad[r, :, C_AT:]
         square[:, C_AT:] += rest * rest
@@ -242,11 +242,11 @@
 
     def trip(it, carry):
         when_in(it, stage_issue)
+        when_in(it - LAG_ZERO - 4 * LAG, stage_five)
+        when_in(it - LAG_ZERO - 3 * LAG, stage_four)
+        when_in(it - LAG_ZERO - 2 * LAG, stage_three)
+        when_in(it - LAG_ZERO - LAG, stage_two)
         when_in(it - LAG_ZERO, stage_one)
-        when_in(it - LAG_ZERO - LAG, stage_two)
-        when_in(it - LAG_ZERO - 2 * LAG, stage_three)
-        when_in(it - LAG_ZERO - 3 * LAG, stage_four)
-        when_in(it - LAG_ZERO - 4 * LAG, stage_five)
 
         @pl.when(it == 5)
         def _():
@@ -294,6 +294,25 @@
     sum_recv[f] = value
     sums = [remote(sum_send, sum_recv.at[f], sum_ssem.at[k], sum_rsem.at[f], dev) for k, dev in enumerate(peers)]
     start(sums)
+    wait_send((norm_zero, norm_one, norm_two, norm_three))
+    pltpu.make_async_copy(norm_d, norm_out, norm_store).wait()
+
+    def drain(slots, copies):
+        def body(j, carry):
+            wait_send(copies(j))
+            return carry
+        lax.fori_loop(total - slots, total, body, 0)
+
+    drain(P_SLOTS, ones)
+    drain(R_SLOTS, lambda j: (zero_copy(emb, 0, j),))
+    drain(SEND_SLOTS, lambda j: twos(j) + (two_c_even(j), three_ab(j), three_c(j), four(j, c_keep)))
+
+    def last(j, carry):
+        out_copy(emb_out, 0, j).wait()
+        return carry
+
+    lax.fori_loop(total - SEND_SLOTS, total, last, 0)
+
     for k in range(1, 8):
         s = lax.rem(f + k, 8)
         remote(sum_send, sum_recv.at[s], sum_ssem.at[0], sum_rsem.at[s], core).wait_recv()
@@ -303,26 +322,7 @@
     scale[...] = jnp.minimum(1.0, CLIP_NORM / jnp.sqrt(whole))
     scale_copy = pltpu.make_async_copy(scale, scale_out, scale_sem)
     scale_copy.start()
-
     wait_send(sums)
-    wait_send((norm_zero, norm_one, norm_two, norm_three))
-    pltpu.make_async_copy(norm_d, norm_out, norm_store).wait()
-
-    def drain(slots, copies):
-        def body(j, carry):
-            wait_send(copies(j))
-            return carry
-        lax.fori_loop(total - slots, total, body, 0)
-
-    drain(P_SLOTS, ones)
-    drain(R_SLOTS, lambda j: (zero_copy(emb, 0, j),))
-    drain(SEND_SLOTS, lambda j: twos(j) + (two_c_even(j), three_ab(j), three_c(j), four(j, c_keep)))
-
-    def last(j, carry):
-        out_copy(emb_out, 0, j).wait()
-        return carry
-
-    lax.fori_loop(total - SEND_SLOTS, total, last, 0)
     scale_copy.wait()
 
 
@@ -369,7 +369,7 @@
         out_specs=(hbm,) * 4,
         scratch_shapes=scratch,
         compiler_params=pltpu.CompilerParams(
-            collective_id=0, has_side_effects=True, vmem_limit_bytes=25 * 1024 * 1024
+            collective_id=0, has_side_effects=True, vmem_limit_bytes=28 * 1024 * 1024
         ),
         name="reduce_grads",
     )(*(pltpu.with_memory_space_constraint(grad, pltpu.HBM) for grad in (

time: 274 us -> 271 us (0.989)
  Pallas kernels: 273 us -> 270 us
where the time goes in v5:
time: 271 us
  Pallas kernels  270 us (100%)
    pallas_call x1, Pallas kernels, reduce_grads(): pl.pallas_call(functools.partial(reduce_kernel, counts), out_shape=(jax.S...  260 us
    pallas_call x1, Pallas kernels, adamw(): pl.pallas_call(adamw_kernel, out_shape=tuple(shapes), in_specs=[vmem] * 1...  9.94 us

profile of v5, /device:TPU:0, one launch (start us, length us, event | category | flops | bytes accessed | tf_op | source)
XLA Modules:
  0.0 271.2 jit_solution(2424616668828542585)
XLA Ops:
  0.6 0.0 copy-start
  0.7 0.0 copy-start.1
  0.7 0.0 copy-start.2
  0.7 0.0 copy-start.3
  0.7 0.0 copy-start.4
  0.7 0.0 copy-start.5
  0.7 0.0 copy-start.6
  0.7 0.0 copy-start.7
  0.7 0.0 copy-start.8
  0.7 260.4 %reduce_grads.1 = (f32[256,5376]{1,0:T(8,128)S(1)}, f32[128,5376]{1,0:T(8,128)S(1)}, f32[16,768]{1,0:T(8,128)S(1)}, f32[8,128]{1,0:T(8,128)S(1)}) custom-call(f32[2,2,2,256,5376]{4,3,2,1,0:T(8,128)} %bitcast.3, f32[2,2,2,128,5376]{4,3,2,1,0:T(8,128)} %bitcast.4, f32[9,1,5376]{2,1,0:T(1,128)} %bitcast.5), custom_call_target="tpu_custom_call" | custom-call | tf_op jit(solution)/shard_map/reduce_grads/pallas_call | solution.py:360
  261.2 0.0 copy-done
  261.2 0.0 copy-done.1
  261.2 0.0 copy-done.2
  261.2 0.0 copy-done.3
  261.2 0.0 copy-done.4
  261.2 0.0 copy-done.5
  261.2 0.0 copy-done.6
  261.3 0.0 copy-done.7
  261.3 0.0 copy-done.8
  261.3 9.9 %adamw.1 = (f32[256,5376]{1,0:T(8,128)}, f32[256,5376]{1,0:T(8,128)}, f32[256,5376]{1,0:T(8,128)}, bf16[256,5376]{1,0:T(8,128)(2,1)}, f32[128,5376]{1,0:T(8,128)...) custom-call(f32[8,128]{1,0:T(8,128)S(1)} %get-tuple-element.16.scale, ...), custom_call_target="tpu_custom_call" | custom-call | flops 41287680 | bytes 61931520 | tf_op jit(solution)/shard_map/adamw/pallas_call | solution.py:458
Async XLA Ops:
  0.6 260.5 %copy-start = (f32[256,5376]{1,0:T(8,128)S(1)}, f32[256,5376]{1,0:T(8,128)}, u32[]{:S(2)}) copy-start(f32[256,5376]{1,0:T(8,128)} %ep.1) | copy-start | bytes 16515076
  0.7 260.5 %copy-start.1 = (f32[256,5376]{1,0:T(8,128)S(1)}, f32[256,5376]{1,0:T(8,128)}, u32[]{:S(2)}) copy-start(f32[256,5376]{1,0:T(8,128)} %em.1) | copy-start | bytes 16515076
  0.7 260.5 %copy-start.2 = (f32[256,5376]{1,0:T(8,128)S(1)}, f32[256,5376]{1,0:T(8,128)}, u32[]{:S(2)}) copy-start(f32[256,5376]{1,0:T(8,128)} %ev.1) | copy-start | bytes 16515076
  0.7 260.5 %copy-start.3 = (f32[128,5376]{1,0:T(8,128)S(1)}, f32[128,5376]{1,0:T(8,128)}, u32[]{:S(2)}) copy-start(f32[128,5376]{1,0:T(8,128)} %mp.1) | copy-start | bytes 8257540
  0.7 260.5 %copy-start.4 = (f32[128,5376]{1,0:T(8,128)S(1)}, f32[128,5376]{1,0:T(8,128)}, u32[]{:S(2)}) copy-start(f32[128,5376]{1,0:T(8,128)} %mm.1) | copy-start | bytes 8257540
  0.7 260.5 %copy-start.5 = (f32[128,5376]{1,0:T(8,128)S(1)}, f32[128,5376]{1,0:T(8,128)}, u32[]{:S(2)}) copy-start(f32[128,5376]{1,0:T(8,128)} %mv.1) | copy-start | bytes 8257540
  0.7 260.5 %copy-start.6 = (f32[9,672]{1,0:T(8,128)S(1)}, f32[9,672]{1,0:T(8,128)}, u32[]{:S(2)}) copy-start(f32[9,672]{1,0:T(8,128)} %np_.1) | copy-start | bytes 72580
  0.7 260.5 %copy-start.7 = (f32[9,672]{1,0:T(8,128)S(1)}, f32[9,672]{1,0:T(8,128)}, u32[]{:S(2)}) copy-start(f32[9,672]{1,0:T(8,128)} %nm.1) | copy-start | bytes 72580
  0.7 260.5 %copy-start.8 = (f32[9,672]{1,0:T(8,128)S(1)}, f32[9,672]{1,0:T(8,128)}, u32[]{:S(2)}) copy-start(f32[9,672]{1,0:T(8,128)} %nv.1) | copy-start | bytes 72580

commit v6 on v5

--- a/solution.py
+++ b/solution.py
@@ -30,7 +30,7 @@
 B_AT = A_COLS
 C_AT = A_COLS + B_COLS
 LAG_ZERO = 3
-LAG = 3
+LAG = 2
 P_SLOTS = 10
 R_SLOTS = 6
 SEND_SLOTS = 8
@@ -39,10 +39,10 @@
 
 def reduce_kernel(counts, emb, mat, norm, emb_out, mat_out, norm_out, scale_out,
                   part, recv_zero, xa, yb, zc, mid, wc, tc, grad, square,
-                  norm_in, norm_part, norm_a, norm_b, norm_c, norm_d, sum_send, sum_recv, scale,
+                  norm_in, norm_part, norm_a, norm_b, norm_c, norm_d, sum_send, sum_recv,
                   load_sem, zero_send, zero_recv, credit,
                   one_send, one_recv, two_send, two_recv, three_send, three_recv, four_send, four_recv, out_sem,
-                  norm_load, norm_send, norm_recv, norm_store, sum_ssem, sum_rsem, scale_sem):
+                  norm_load, norm_send, norm_recv, sum_ssem, sum_rsem):
     emb_count, mat_count = counts
     total = emb_count + mat_count
     z = lax.axis_index("dp")
@@ -67,7 +67,7 @@
     a_cols, b_cols, ab_cols = pl.ds(0, A_COLS), pl.ds(B_AT, B_COLS), pl.ds(0, C_AT)
 
     barrier = pltpu.get_barrier_semaphore()
-    for dev in peers + [zn]:
+    for dev in (core, xn, yn, zn):
         pl.semaphore_signal(barrier, inc=1, device_id=dev, device_id_type=MESH)
     norm_copy = pltpu.make_async_copy(norm, norm_in, norm_load)
     norm_copy.start()
@@ -167,7 +167,10 @@
         def _():
             pl.semaphore_signal(credit, inc=1, device_id=core, device_id_type=MESH)
 
-        start(ones(j))
+        start(ones(j)[:1])
+
+    def stage_one_more(j):
+        start(ones(j)[1:])
 
     def stage_two(j):
         s, r = lax.rem(j, P_SLOTS), lax.rem(j, RING)
@@ -242,11 +245,12 @@
 
     def trip(it, carry):
         when_in(it, stage_issue)
+        when_in(it - LAG_ZERO, stage_one)
         when_in(it - LAG_ZERO - 4 * LAG, stage_five)
         when_in(it - LAG_ZERO - 3 * LAG, stage_four)
         when_in(it - LAG_ZERO - 2 * LAG, stage_three)
         when_in(it - LAG_ZERO - LAG, stage_two)
-        when_in(it - LAG_ZERO, stage_one)
+        when_in(it - LAG_ZERO, stage_one_more)
 
         @pl.when(it == 5)
         def _():
@@ -278,13 +282,13 @@
         def _():
             norm_three.wait_recv()
             norm_d[...] = (norm_d[...] + norm_c[...]) * (1.0 / 16.0)
-            pltpu.make_async_copy(norm_d, norm_out, norm_store).start()
+            norm_out[...] = norm_d[...]
 
         return carry
 
-    pl.semaphore_wait(barrier, 8)
     norm_part[...] = jnp.zeros_like(norm_part)
     square[...] = jnp.zeros_like(square)
+    pl.semaphore_wait(barrier, 4)
     lax.fori_loop(0, total + LAG_ZERO + 4 * LAG, trip, 0)
 
     norm_sq = norm_d[...] * norm_d[...]
@@ -295,7 +299,6 @@
     sums = [remote(sum_send, sum_recv.at[f], sum_ssem.at[k], sum_rsem.at[f], dev) for k, dev in enumerate(peers)]
     start(sums)
     wait_send((norm_zero, norm_one, norm_two, norm_three))
-    pltpu.make_async_copy(norm_d, norm_out, norm_store).wait()
 
     def drain(slots, copies):
         def body(j, carry):
@@ -319,11 +322,8 @@
     whole = sum_recv[0]
     for k in range(1, 8):
         whole = whole + sum_recv[k]
-    scale[...] = jnp.minimum(1.0, CLIP_NORM / jnp.sqrt(whole))
-    scale_copy = pltpu.make_async_copy(scale, scale_out, scale_sem)
-    scale_copy.start()
+    scale_out[...] = jnp.minimum(1.0, CLIP_NORM / jnp.sqrt(whole))
     wait_send(sums)
-    scale_copy.wait()
 
 
 def reduce_grads(emb_grad, mat_grad, norm_grad):
@@ -350,13 +350,13 @@
         pltpu.VMEM(NORM_PAD, F32),
         pltpu.VMEM((8, 128), F32),
         pltpu.VMEM((8, 8, 128), F32),
-        pltpu.VMEM((8, 128), F32),
         dma((P_SLOTS,)), dma((R_SLOTS,)), dma((R_SLOTS,)), pltpu.SemaphoreType.REGULAR,
         dma((3, P_SLOTS)), dma((3, RING)), dma((3, SEND_SLOTS)), dma((3, RING)),
         dma((2, SEND_SLOTS)), dma((2, RING)), dma((SEND_SLOTS,)), dma((RING,)), dma((SEND_SLOTS,)),
-        dma, dma((4,)), dma((4,)), dma, dma((7,)), dma((8,)), dma,
+        dma, dma((4,)), dma((4,)), dma((7,)), dma((8,)),
     ]
     hbm = pl.BlockSpec(memory_space=pl.ANY)
+    vmem = pl.BlockSpec(memory_space=pltpu.VMEM)
     return pl.pallas_call(
         functools.partial(reduce_kernel, counts),
         out_shape=(
@@ -366,7 +366,7 @@
             jax.ShapeDtypeStruct((8, 128), F32),
         ),
         in_specs=[pl.BlockSpec(memory_space=pltpu.HBM)] * 3,
-        out_specs=(hbm,) * 4,
+        out_specs=(hbm, hbm, vmem, vmem),
         scratch_shapes=scratch,
         compiler_params=pltpu.CompilerParams(
             collective_id=0, has_side_effects=True, vmem_limit_bytes=28 * 1024 * 1024

time: 271 us -> 270 us (level)
  no operation moved by 1% of the time
where the time goes in v6:
time: 270 us
  Pallas kernels  269 us (100%)
    pallas_call x1, Pallas kernels, reduce_grads(): pl.pallas_call(functools.partial(reduce_kernel, counts), out_shape=(jax.S...  259 us
    pallas_call x1, Pallas kernels, adamw(): pl.pallas_call(adamw_kernel, out_shape=tuple(shapes), in_specs=[vmem] * 1...  9.94 us

profile of v6, /device:TPU:0, one launch (start us, length us, event | category | flops | bytes accessed | tf_op | source)
XLA Modules:
  0.0 269.7 jit_solution(18028798103577611304)
XLA Ops:
  0.6 0.0 copy-start
  0.7 0.0 copy-start.1
  0.7 0.0 copy-start.2
  0.7 0.0 copy-start.3
  0.7 0.0 copy-start.4
  0.7 0.0 copy-start.5
  0.7 0.0 copy-start.6
  0.7 0.0 copy-start.7
  0.7 0.0 copy-start.8
  0.7 258.9 %reduce_grads.1 = (f32[256,5376]{1,0:T(8,128)S(1)}, f32[128,5376]{1,0:T(8,128)S(1)}, f32[16,768]{1,0:T(8,128)S(1)}, f32[8,128]{1,0:T(8,128)S(1)}) custom-call(f32[2,2,2,256,5376]{4,3,2,1,0:T(8,128)} %bitcast.3, f32[2,2,2,128,5376]{4,3,2,1,0:T(8,128)} %bitcast.4, f32[9,1,5376]{2,1,0:T(1,128)} %bitcast.5), custom_call_target="tpu_custom_call" | custom-call | tf_op jit(solution)/shard_map/reduce_grads/pallas_call | solution.py:360
  259.7 0.0 copy-done
  259.7 0.0 copy-done.1
  259.7 0.0 copy-done.2
  259.7 0.0 copy-done.3
  259.7 0.0 copy-done.4
  259.7 0.0 copy-done.5
  259.7 0.0 copy-done.6
  259.7 0.0 copy-done.7
  259.8 0.0 copy-done.8
  259.8 9.9 %adamw.1 = (f32[256,5376]{1,0:T(8,128)}, f32[256,5376]{1,0:T(8,128)}, f32[256,5376]{1,0:T(8,128)}, bf16[256,5376]{1,0:T(8,128)(2,1)}, f32[128,5376]{1,0:T(8,128)...) custom-call(f32[8,128]{1,0:T(8,128)S(1)} %get-tuple-element.16.scale, ...), custom_call_target="tpu_custom_call" | custom-call | flops 41287680 | bytes 61931520 | tf_op jit(solution)/shard_map/adamw/pallas_call | solution.py:458
Async XLA Ops:
  0.6 259.0 %copy-start = (f32[256,5376]{1,0:T(8,128)S(1)}, f32[256,5376]{1,0:T(8,128)}, u32[]{:S(2)}) copy-start(f32[256,5376]{1,0:T(8,128)} %ep.1) | copy-start | bytes 16515076
  0.7 259.0 %copy-start.1 = (f32[256,5376]{1,0:T(8,128)S(1)}, f32[256,5376]{1,0:T(8,128)}, u32[]{:S(2)}) copy-start(f32[256,5376]{1,0:T(8,128)} %em.1) | copy-start | bytes 16515076
  0.7 259.0 %copy-start.2 = (f32[256,5376]{1,0:T(8,128)S(1)}, f32[256,5376]{1,0:T(8,128)}, u32[]{:S(2)}) copy-start(f32[256,5376]{1,0:T(8,128)} %ev.1) | copy-start | bytes 16515076
  0.7 259.0 %copy-start.3 = (f32[128,5376]{1,0:T(8,128)S(1)}, f32[128,5376]{1,0:T(8,128)}, u32[]{:S(2)}) copy-start(f32[128,5376]{1,0:T(8,128)} %mp.1) | copy-start | bytes 8257540
  0.7 259.0 %copy-start.4 = (f32[128,5376]{1,0:T(8,128)S(1)}, f32[128,5376]{1,0:T(8,128)}, u32[]{:S(2)}) copy-start(f32[128,5376]{1,0:T(8,128)} %mm.1) | copy-start | bytes 8257540
  0.7 259.0 %copy-start.5 = (f32[128,5376]{1,0:T(8,128)S(1)}, f32[128,5376]{1,0:T(8,128)}, u32[]{:S(2)}) copy-start(f32[128,5376]{1,0:T(8,128)} %mv.1) | copy-start | bytes 8257540
  0.7 259.0 %copy-start.6 = (f32[9,672]{1,0:T(8,128)S(1)}, f32[9,672]{1,0:T(8,128)}, u32[]{:S(2)}) copy-start(f32[9,672]{1,0:T(8,128)} %np_.1) | copy-start | bytes 72580
  0.7 259.0 %copy-start.7 = (f32[9,672]{1,0:T(8,128)S(1)}, f32[9,672]{1,0:T(8,128)}, u32[]{:S(2)}) copy-start(f32[9,672]{1,0:T(8,128)} %nm.1) | copy-start | bytes 72580
  0.7 259.0 %copy-start.8 = (f32[9,672]{1,0:T(8,128)S(1)}, f32[9,672]{1,0:T(8,128)}, u32[]{:S(2)}) copy-start(f32[9,672]{1,0:T(8,128)} %nv.1) | copy-start | bytes 72580

commit v7 on v6

--- a/solution.py
+++ b/solution.py
@@ -29,7 +29,7 @@
 HALF = 640
 B_AT = A_COLS
 C_AT = A_COLS + B_COLS
-LAG_ZERO = 3
+LAG_ZERO = 1
 LAG = 2
 P_SLOTS = 10
 R_SLOTS = 6
@@ -283,6 +283,8 @@
             norm_three.wait_recv()
             norm_d[...] = (norm_d[...] + norm_c[...]) * (1.0 / 16.0)
             norm_out[...] = norm_d[...]
+            norm_sq = norm_d[...] * norm_d[...]
+            square[:, :NORM_PAD[1]] += norm_sq[:ROWS] + norm_sq[ROWS:]
 
         return carry
 
@@ -291,9 +293,7 @@
     pl.semaphore_wait(barrier, 4)
     lax.fori_loop(0, total + LAG_ZERO + 4 * LAG, trip, 0)
 
-    norm_sq = norm_d[...] * norm_d[...]
-    local = jnp.sum(square[...]) + jnp.sum(norm_sq)
-    value = jnp.full((8, 128), local, F32)
+    value = jnp.full((8, 128), jnp.sum(square[...]), F32)
     sum_send[...] = value
     sum_recv[f] = value
     sums = [remote(sum_send, sum_recv.at[f], sum_ssem.at[k], sum_rsem.at[f], dev) for k, dev in enumerate(peers)]

time: 270 us -> 270 us (level)
  no operation moved by 1% of the time
where the time goes in v7:
time: 270 us; the launch traced here: 269 us
  Pallas kernels  269 us (100%)
    pallas_call x1, Pallas kernels, reduce_grads(): pl.pallas_call(functools.partial(reduce_kernel, counts), out_shape=(jax.S...  259 us
    pallas_call x1, Pallas kernels, adamw(): pl.pallas_call(adamw_kernel, out_shape=tuple(shapes), in_specs=[vmem] * 1...  9.94 us

profile of v7, /device:TPU:0, one launch (start us, length us, event | category | flops | bytes accessed | tf_op | source)
XLA Modules:
  0.0 269.4 jit_solution(11354621478995730227)
XLA Ops:
  0.6 0.0 copy-start
  0.7 0.0 copy-start.1
  0.7 0.0 copy-start.2
  0.7 0.0 copy-start.3
  0.7 0.0 copy-start.4
  0.7 0.0 copy-start.5
  0.7 0.0 copy-start.6
  0.7 0.0 copy-start.7
  0.7 0.0 copy-start.8
  0.7 258.7 %reduce_grads.1 = (f32[256,5376]{1,0:T(8,128)S(1)}, f32[128,5376]{1,0:T(8,128)S(1)}, f32[16,768]{1,0:T(8,128)S(1)}, f32[8,128]{1,0:T(8,128)S(1)}) custom-call(f32[2,2,2,256,5376]{4,3,2,1,0:T(8,128)} %bitcast.3, f32[2,2,2,128,5376]{4,3,2,1,0:T(8,128)} %bitcast.4, f32[9,1,5376]{2,1,0:T(1,128)} %bitcast.5), custom_call_target="tpu_custom_call" | custom-call | tf_op jit(solution)/shard_map/reduce_grads/pallas_call | solution.py:360
  259.4 0.0 copy-done
  259.4 0.0 copy-done.1
  259.4 0.0 copy-done.2
  259.4 0.0 copy-done.3
  259.4 0.0 copy-done.4
  259.5 0.0 copy-done.5
  259.5 0.0 copy-done.6
  259.5 0.0 copy-done.7
  259.5 0.0 copy-done.8
  259.5 9.9 %adamw.1 = (f32[256,5376]{1,0:T(8,128)}, f32[256,5376]{1,0:T(8,128)}, f32[256,5376]{1,0:T(8,128)}, bf16[256,5376]{1,0:T(8,128)(2,1)}, f32[128,5376]{1,0:T(8,128)...) custom-call(f32[8,128]{1,0:T(8,128)S(1)} %get-tuple-element.16.scale, ...), custom_call_target="tpu_custom_call" | custom-call | flops 41287680 | bytes 61931520 | tf_op jit(solution)/shard_map/adamw/pallas_call | solution.py:458
Async XLA Ops:
  0.6 258.8 %copy-start = (f32[256,5376]{1,0:T(8,128)S(1)}, f32[256,5376]{1,0:T(8,128)}, u32[]{:S(2)}) copy-start(f32[256,5376]{1,0:T(8,128)} %ep.1) | copy-start | bytes 16515076
  0.7 258.8 %copy-start.1 = (f32[256,5376]{1,0:T(8,128)S(1)}, f32[256,5376]{1,0:T(8,128)}, u32[]{:S(2)}) copy-start(f32[256,5376]{1,0:T(8,128)} %em.1) | copy-start | bytes 16515076
  0.7 258.8 %copy-start.2 = (f32[256,5376]{1,0:T(8,128)S(1)}, f32[256,5376]{1,0:T(8,128)}, u32[]{:S(2)}) copy-start(f32[256,5376]{1,0:T(8,128)} %ev.1) | copy-start | bytes 16515076
  0.7 258.8 %copy-start.3 = (f32[128,5376]{1,0:T(8,128)S(1)}, f32[128,5376]{1,0:T(8,128)}, u32[]{:S(2)}) copy-start(f32[128,5376]{1,0:T(8,128)} %mp.1) | copy-start | bytes 8257540
  0.7 258.8 %copy-start.4 = (f32[128,5376]{1,0:T(8,128)S(1)}, f32[128,5376]{1,0:T(8,128)}, u32[]{:S(2)}) copy-start(f32[128,5376]{1,0:T(8,128)} %mm.1) | copy-start | bytes 8257540
  0.7 258.8 %copy-start.5 = (f32[128,5376]{1,0:T(8,128)S(1)}, f32[128,5376]{1,0:T(8,128)}, u32[]{:S(2)}) copy-start(f32[128,5376]{1,0:T(8,128)} %mv.1) | copy-start | bytes 8257540
  0.7 258.8 %copy-start.6 = (f32[9,672]{1,0:T(8,128)S(1)}, f32[9,672]{1,0:T(8,128)}, u32[]{:S(2)}) copy-start(f32[9,672]{1,0:T(8,128)} %np_.1) | copy-start | bytes 72580
  0.7 258.8 %copy-start.7 = (f32[9,672]{1,0:T(8,128)S(1)}, f32[9,672]{1,0:T(8,128)}, u32[]{:S(2)}) copy-start(f32[9,672]{1,0:T(8,128)} %nm.1) | copy-start | bytes 72580
  0.7 258.8 %copy-start.8 = (f32[9,672]{1,0:T(8,128)S(1)}, f32[9,672]{1,0:T(8,128)}, u32[]{:S(2)}) copy-start(f32[9,672]{1,0:T(8,128)} %nv.1) | copy-start | bytes 72580

commit v8 on v7

--- a/solution.py
+++ b/solution.py
@@ -30,7 +30,7 @@
 B_AT = A_COLS
 C_AT = A_COLS + B_COLS
 LAG_ZERO = 1
-LAG = 2
+LAG = 3
 P_SLOTS = 10
 R_SLOTS = 6
 SEND_SLOTS = 8

time: 270 us -> 269 us (level)
  no operation moved by 1% of the time
where the time goes in v8:
time: 269 us
  Pallas kernels  268 us (100%)
    pallas_call x1, Pallas kernels, reduce_grads(): pl.pallas_call(functools.partial(reduce_kernel, counts), out_shape=(jax.S...  258 us
    pallas_call x1, Pallas kernels, adamw(): pl.pallas_call(adamw_kernel, out_shape=tuple(shapes), in_specs=[vmem] * 1...  9.94 us

profile of v8, /device:TPU:0, one launch (start us, length us, event | category | flops | bytes accessed | tf_op | source)
XLA Modules:
  0.0 269.2 jit_solution(12620963938407101799)
XLA Ops:
  0.6 0.0 copy-start
  0.7 0.0 copy-start.1
  0.7 0.0 copy-start.2
  0.7 0.0 copy-start.3
  0.7 0.0 copy-start.4
  0.7 0.0 copy-start.5
  0.7 0.0 copy-start.6
  0.7 0.0 copy-start.7
  0.7 0.0 copy-start.8
  0.7 258.4 %reduce_grads.1 = (f32[256,5376]{1,0:T(8,128)S(1)}, f32[128,5376]{1,0:T(8,128)S(1)}, f32[16,768]{1,0:T(8,128)S(1)}, f32[8,128]{1,0:T(8,128)S(1)}) custom-call(f32[2,2,2,256,5376]{4,3,2,1,0:T(8,128)} %bitcast.3, f32[2,2,2,128,5376]{4,3,2,1,0:T(8,128)} %bitcast.4, f32[9,1,5376]{2,1,0:T(1,128)} %bitcast.5), custom_call_target="tpu_custom_call" | custom-call | tf_op jit(solution)/shard_map/reduce_grads/pallas_call | solution.py:360
  259.2 0.0 copy-done
  259.2 0.0 copy-done.1
  259.2 0.0 copy-done.2
  259.2 0.0 copy-done.3
  259.2 0.0 copy-done.4
  259.2 0.0 copy-done.5
  259.2 0.0 copy-done.6
  259.3 0.0 copy-done.7
  259.3 0.0 copy-done.8
  259.3 9.9 %adamw.1 = (f32[256,5376]{1,0:T(8,128)}, f32[256,5376]{1,0:T(8,128)}, f32[256,5376]{1,0:T(8,128)}, bf16[256,5376]{1,0:T(8,128)(2,1)}, f32[128,5376]{1,0:T(8,128)...) custom-call(f32[8,128]{1,0:T(8,128)S(1)} %get-tuple-element.16.scale, ...), custom_call_target="tpu_custom_call" | custom-call | flops 41287680 | bytes 61931520 | tf_op jit(solution)/shard_map/adamw/pallas_call | solution.py:458
Async XLA Ops:
  0.6 258.5 %copy-start = (f32[256,5376]{1,0:T(8,128)S(1)}, f32[256,5376]{1,0:T(8,128)}, u32[]{:S(2)}) copy-start(f32[256,5376]{1,0:T(8,128)} %ep.1) | copy-start | bytes 16515076
  0.7 258.5 %copy-start.1 = (f32[256,5376]{1,0:T(8,128)S(1)}, f32[256,5376]{1,0:T(8,128)}, u32[]{:S(2)}) copy-start(f32[256,5376]{1,0:T(8,128)} %em.1) | copy-start | bytes 16515076
  0.7 258.5 %copy-start.2 = (f32[256,5376]{1,0:T(8,128)S(1)}, f32[256,5376]{1,0:T(8,128)}, u32[]{:S(2)}) copy-start(f32[256,5376]{1,0:T(8,128)} %ev.1) | copy-start | bytes 16515076
  0.7 258.5 %copy-start.3 = (f32[128,5376]{1,0:T(8,128)S(1)}, f32[128,5376]{1,0:T(8,128)}, u32[]{:S(2)}) copy-start(f32[128,5376]{1,0:T(8,128)} %mp.1) | copy-start | bytes 8257540
  0.7 258.5 %copy-start.4 = (f32[128,5376]{1,0:T(8,128)S(1)}, f32[128,5376]{1,0:T(8,128)}, u32[]{:S(2)}) copy-start(f32[128,5376]{1,0:T(8,128)} %mm.1) | copy-start | bytes 8257540
  0.7 258.5 %copy-start.5 = (f32[128,5376]{1,0:T(8,128)S(1)}, f32[128,5376]{1,0:T(8,128)}, u32[]{:S(2)}) copy-start(f32[128,5376]{1,0:T(8,128)} %mv.1) | copy-start | bytes 8257540
  0.7 258.5 %copy-start.6 = (f32[9,672]{1,0:T(8,128)S(1)}, f32[9,672]{1,0:T(8,128)}, u32[]{:S(2)}) copy-start(f32[9,672]{1,0:T(8,128)} %np_.1) | copy-start | bytes 72580
  0.7 258.5 %copy-start.7 = (f32[9,672]{1,0:T(8,128)S(1)}, f32[9,672]{1,0:T(8,128)}, u32[]{:S(2)}) copy-start(f32[9,672]{1,0:T(8,128)} %nm.1) | copy-start | bytes 72580
  0.7 258.5 %copy-start.8 = (f32[9,672]{1,0:T(8,128)S(1)}, f32[9,672]{1,0:T(8,128)}, u32[]{:S(2)}) copy-start(f32[9,672]{1,0:T(8,128)} %nv.1) | copy-start | bytes 72580

commit v9 on v7

--- a/solution.py
+++ b/solution.py
@@ -24,17 +24,16 @@
 NORM_COLS = 672
 NORM_PAD = (16, 768)
 ROWS = 8
-A_COLS = 2048
-B_COLS = 2048
-HALF = 640
-B_AT = A_COLS
-C_AT = A_COLS + B_COLS
+PLANS = ((1920, 768), (2176, 512))
+INNER = (20, 44)
+SIDE_MAX = max(side for side, _ in PLANS)
+HALF_MAX = max(half for _, half in PLANS)
 LAG_ZERO = 1
 LAG = 2
 P_SLOTS = 10
 R_SLOTS = 6
 SEND_SLOTS = 8
-RING = 20
+RING = 16
 
 
 def reduce_kernel(counts, emb, mat, norm, emb_out, mat_out, norm_out, scale_out,
@@ -60,11 +59,13 @@
         return pltpu.make_async_remote_copy(src_ref=src, dst_ref=dst, send_sem=ssem, recv_sem=rsem,
                                             device_id=dev, device_id_type=MESH)
 
-    def half_at(base, which):
-        return pl.ds(pl.multiple_of(base + which * HALF, 128), HALF)
-
-    c_keep, c_give = half_at(C_AT, z), half_at(C_AT, 1 - z)
-    a_cols, b_cols, ab_cols = pl.ds(0, A_COLS), pl.ds(B_AT, B_COLS), pl.ds(0, C_AT)
+    def on_plan(j, body):
+        inner = jnp.logical_and(j >= INNER[0], j < INNER[1])
+        pl.when(jnp.logical_not(inner))(lambda: body(j, *PLANS[0]))
+        pl.when(inner)(lambda: body(j, *PLANS[1]))
+
+    def half_at(side, half, which):
+        return pl.ds(pl.multiple_of(2 * side + which * half, 128), half)
 
     barrier = pltpu.get_barrier_semaphore()
     for dev in (core, xn, yn, zn):
@@ -89,38 +90,39 @@
         s = lax.rem(j, R_SLOTS)
         return remote(ref.at[:, :, 1 - c, pl.ds(row, ROWS), :], recv_zero.at[s], zero_send.at[s], zero_recv.at[s], core)
 
-    def ones(j):
+    def ones(j, side, half):
         s, r = lax.rem(j, P_SLOTS), lax.rem(j, RING)
-        return (remote(part.at[s, :, :, :, c_give], zc.at[r], one_send.at[2, s], one_recv.at[2, r], zn),
-                remote(part.at[s, :, 1 - x, :, a_cols], xa.at[r], one_send.at[0, s], one_recv.at[0, r], xn),
-                remote(part.at[s, 1 - y, :, :, b_cols], yb.at[r], one_send.at[1, s], one_recv.at[1, r], yn))
-
-    def two_c_even(j):
+        return (remote(part.at[s, :, :, :, half_at(side, half, 1 - z)], zc.at[r, :, :, :, :half], one_send.at[2, s], one_recv.at[2, r], zn),
+                remote(part.at[s, :, 1 - x, :, :side], xa.at[r, :, :, :side], one_send.at[0, s], one_recv.at[0, r], xn),
+                remote(part.at[s, 1 - y, :, :, side:2 * side], yb.at[r, :, :, :side], one_send.at[1, s], one_recv.at[1, r], yn))
+
+    def two_c_even(j, side, half):
         s, r = lax.rem(j, SEND_SLOTS), lax.rem(j, RING)
-        return remote(zc.at[r, :, 1 - x], wc.at[r], two_send.at[2, s], two_recv.at[2, r], xn)
-
-    def two_c_odd(j):
+        return remote(zc.at[r, :, 1 - x, :, :half], wc.at[r, :, :, :half], two_send.at[2, s], two_recv.at[2, r], xn)
+
+    def two_c_odd(j, side, half):
         s, r = lax.rem(j, SEND_SLOTS), lax.rem(j, RING)
-        return remote(zc.at[r, 1 - y], wc.at[r], two_send.at[2, s], two_recv.at[2, r], yn)
-
-    def twos(j):
+        return remote(zc.at[r, 1 - y, :, :, :half], wc.at[r, :, :, :half], two_send.at[2, s], two_recv.at[2, r], yn)
+
+    def twos(j, side, half):
         s, r = lax.rem(j, SEND_SLOTS), lax.rem(j, RING)
-        return (remote(xa.at[r, 1 - y], mid.at[r, :, a_cols], two_send.at[0, s], two_recv.at[0, r], yn),
-                remote(yb.at[r, 1 - x], mid.at[r, :, b_cols], two_send.at[1, s], two_recv.at[1, r], xn))
-
-    def three_c(j):
+        return (remote(xa.at[r, 1 - y, :, :side], mid.at[r, :, :side], two_send.at[0, s], two_recv.at[0, r], yn),
+                remote(yb.at[r, 1 - x, :, :side], mid.at[r, :, side:2 * side], two_send.at[1, s], two_recv.at[1, r], xn))
+
+    def three_c(j, side, half):
         s, r, odd = lax.rem(j, SEND_SLOTS), lax.rem(j, RING), lax.rem(j, 2)
         here = y + odd * (x - y)
         step = (4 - 8 * y) + odd * ((2 - 4 * x) - (4 - 8 * y))
-        return remote(wc.at[r, 1 - here], tc.at[r], three_send.at[1, s], three_recv.at[1, r], (z, f + step))
-
-    def three_ab(j):
+        return remote(wc.at[r, 1 - here, :, :half], tc.at[r, :, :half], three_send.at[1, s], three_recv.at[1, r], (z, f + step))
+
+    def three_ab(j, side, half):
         s, r = lax.rem(j, SEND_SLOTS), lax.rem(j, RING)
-        return remote(mid.at[r], grad.at[r, :, ab_cols], three_send.at[0, s], three_recv.at[0, r], zn)
-
-    def four(j, c_at):
+        return remote(mid.at[r, :, :2 * side], grad.at[r, :, :2 * side], three_send.at[0, s], three_recv.at[0, r], zn)
+
+    def four(j, side, half, which):
         s, r = lax.rem(j, SEND_SLOTS), lax.rem(j, RING)
-        return remote(grad.at[r, :, c_at], grad.at[r, :, c_at], four_send.at[s], four_recv.at[r], zn)
+        cols = half_at(side, half, which)
+        return remote(grad.at[r, :, cols], grad.at[r, :, cols], four_send.at[s], four_recv.at[r], zn)
 
     def out_copy(ref, row, j):
         return pltpu.make_async_copy(grad.at[lax.rem(j, RING)], ref.at[pl.ds(row, ROWS), :],
@@ -134,6 +136,11 @@
     def when_in(j, body):
         pl.when(jnp.logical_and(j >= 0, j < total))(functools.partial(body, j))
 
+    def after(j, slots, copies):
+        @pl.when(j >= slots)
+        def _():
+            on_plan(j - slots, lambda *args: wait_send(copies(*args)))
+
     def start(copies):
         for copy in copies:
             copy.start()
@@ -143,9 +150,7 @@
             copy.wait_send()
 
     def stage_issue(j):
-        @pl.when(j >= P_SLOTS)
-        def _():
-            wait_send(ones(j - P_SLOTS))
+        after(j, P_SLOTS, ones)
 
         @pl.when(j >= R_SLOTS)
         def _():
@@ -167,81 +172,84 @@
         def _():
             pl.semaphore_signal(credit, inc=1, device_id=core, device_id_type=MESH)
 
-        start(ones(j)[:1])
+        on_plan(j, lambda *args: start(ones(*args)[:1]))
 
     def stage_one_more(j):
-        start(ones(j)[1:])
+        on_plan(j, lambda *args: start(ones(*args)[1:]))
 
     def stage_two(j):
-        s, r = lax.rem(j, P_SLOTS), lax.rem(j, RING)
-        even = lax.rem(j, 2) == 0
-        for copy in ones(j):
-            copy.wait_recv()
-        zc[r] += part[s, :, :, :, c_keep]
-        xa[r] += part[s, :, x, :, a_cols]
-        yb[r] += part[s, y, :, :, b_cols]
+        after(j, SEND_SLOTS, lambda *args: twos(*args) + (two_c_even(*args),))
+
+        def body(j, side, half):
+            s, r = lax.rem(j, P_SLOTS), lax.rem(j, RING)
+            even = lax.rem(j, 2) == 0
+            for copy in ones(j, side, half):
+                copy.wait_recv()
+            zc[r, :, :, :, :half] += part[s, :, :, :, half_at(side, half, z)]
+            xa[r, :, :, :side] += part[s, :, x, :, :side]
+            yb[r, :, :, :side] += part[s, y, :, :, side:2 * side]
+            pl.when(even)(lambda: two_c_even(j, side, half).start())
+            pl.when(jnp.logical_not(even))(lambda: two_c_odd(j, side, half).start())
+            start(twos(j, side, half))
+
+        on_plan(j, body)
+
+    def stage_three(j):
+        after(j, SEND_SLOTS, lambda *args: (three_ab(*args), three_c(*args)))
+
+        def body(j, side, half):
+            r = lax.rem(j, RING)
+            even = lax.rem(j, 2) == 0
+            for copy in twos(j, side, half) + (two_c_even(j, side, half),):
+                copy.wait_recv()
+
+            @pl.when(even)
+            def _():
+                wc[r, :, :, :half] += zc[r, :, x, :, :half]
+
+            @pl.when(jnp.logical_not(even))
+            def _():
+                wc[r, :, :, :half] += zc[r, y, :, :, :half]
+
+            mid[r, :, :side] += xa[r, y, :, :side]
+            mid[r, :, side:2 * side] += yb[r, x, :, :side]
+            start((three_c(j, side, half), three_ab(j, side, half)))
+
+        on_plan(j, body)
+
+    def stage_four(j):
+        after(j, SEND_SLOTS, lambda *args: (four(*args, z),))
+
+        def body(j, side, half):
+            r, odd = lax.rem(j, RING), lax.rem(j, 2)
+            here = y + odd * (x - y)
+            three_c(j, side, half).wait_recv()
+            grad[r, :, half_at(side, half, z)] = (tc[r, :, :half] + wc[r, here, :, :half]) * (1.0 / 16.0)
+            four(j, side, half, z).start()
+
+        on_plan(j, body)
+
+    def stage_five(j):
+        def body(j, side, half):
+            r = lax.rem(j, RING)
+            three_ab(j, side, half).wait_recv()
+            both = (grad[r, :, :2 * side] + mid[r, :, :2 * side]) * (1.0 / 16.0)
+            grad[r, :, :2 * side] = both
+            square[:, :2 * side] += both * both
+            four(j, side, half, 1 - z).wait_recv()
+            rest = grad[r, :, 2 * side:]
+            square[:, 2 * side:] += rest * rest
+
+        on_plan(j, body)
 
         @pl.when(j >= SEND_SLOTS)
         def _():
-            wait_send(twos(j - SEND_SLOTS) + (two_c_even(j - SEND_SLOTS),))
-
-        pl.when(even)(lambda: two_c_even(j).start())
-        pl.when(jnp.logical_not(even))(lambda: two_c_odd(j).start())
-        start(twos(j))
-
-    def stage_three(j):
-        r = lax.rem(j, RING)
-        even = lax.rem(j, 2) == 0
-        for copy in twos(j) + (two_c_even(j),):
-            copy.wait_recv()
-
-        @pl.when(even)
-        def _():
-            wc[r] += zc[r, :, x]
-
-        @pl.when(jnp.logical_not(even))
-        def _():
-            wc[r] += zc[r, y]
-
-        mid[r, :, a_cols] += xa[r, y]
-        mid[r, :, b_cols] += yb[r, x]
-
-        @pl.when(j >= SEND_SLOTS)
-        def _():
-            wait_send((three_ab(j - SEND_SLOTS), three_c(j - SEND_SLOTS)))
-
-        start((three_c(j), three_ab(j)))
-
-    def stage_four(j):
-        r, odd = lax.rem(j, RING), lax.rem(j, 2)
-        here = y + odd * (x - y)
-        three_c(j).wait_recv()
-
-        @pl.when(j >= SEND_SLOTS)
-        def _():
-            four(j - SEND_SLOTS, c_keep).wait_send()
-
-        grad[r, :, c_keep] = (tc[r] + wc[r, here]) * (1.0 / 16.0)
-        four(j, c_keep).start()
-
-    def stage_five(j):
-        r = lax.rem(j, RING)
-        three_ab(j).wait_recv()
-        both = (grad[r, :, ab_cols] + mid[r]) * (1.0 / 16.0)
-        grad[r, :, ab_cols] = both
-        square[:, ab_cols] += both * both
-        four(j, c_give).wait_recv()
-        rest = grad[r, :, C_AT:]
-        square[:, C_AT:] += rest * rest
-
-        @pl.when(j >= SEND_SLOTS)
-        def _():
             out_copy(emb_out, 0, j - SEND_SLOTS).wait()
 
-        def body(_, ref, row):
+        def store(_, ref, row):
             out_copy(ref, row, j).start()
 
-        on_rows(j, body)
+        on_rows(j, store)
 
     def trip(it, carry):
         when_in(it, stage_issue)
@@ -302,13 +310,13 @@
 
     def drain(slots, copies):
         def body(j, carry):
-            wait_send(copies(j))
+            on_plan(j, lambda *args: wait_send(copies(*args)))
             return carry
         lax.fori_loop(total - slots, total, body, 0)
 
     drain(P_SLOTS, ones)
-    drain(R_SLOTS, lambda j: (zero_copy(emb, 0, j),))
-    drain(SEND_SLOTS, lambda j: twos(j) + (two_c_even(j), three_ab(j), three_c(j), four(j, c_keep)))
+    drain(R_SLOTS, lambda j, side, half: (zero_copy(emb, 0, j),))
+    drain(SEND_SLOTS, lambda *args: twos(*args) + (two_c_even(*args), three_ab(*args), three_c(*args), four(*args, z)))
 
     def last(j, carry):
         out_copy(emb_out, 0, j).wait()
@@ -334,12 +342,12 @@
     scratch = [
         pltpu.VMEM((P_SLOTS, 2, 2, ROWS, WIDTH), F32),
         pltpu.VMEM((R_SLOTS, 2, 2, ROWS, WIDTH), F32),
-        pltpu.VMEM((RING, 2, ROWS, A_COLS), F32),
-        pltpu.VMEM((RING, 2, ROWS, B_COLS), F32),
-        pltpu.VMEM((RING, 2, 2, ROWS, HALF), F32),
-        pltpu.VMEM((RING, ROWS, C_AT), F32),
-        pltpu.VMEM((RING, 2, ROWS, HALF), F32),
-        pltpu.VMEM((RING, ROWS, HALF), F32),
+        pltpu.VMEM((RING, 2, ROWS, SIDE_MAX), F32),
+        pltpu.VMEM((RING, 2, ROWS, SIDE_MAX), F32),
+        pltpu.VMEM((RING, 2, 2, ROWS, HALF_MAX), F32),
+        pltpu.VMEM((RING, ROWS, 2 * SIDE_MAX), F32),
+        pltpu.VMEM((RING, 2, ROWS, HALF_MAX), F32),
+        pltpu.VMEM((RING, ROWS, HALF_MAX), F32),
         pltpu.VMEM((RING, ROWS, WIDTH), F32),
         pltpu.VMEM((ROWS, WIDTH), F32),
         pltpu.VMEM((NORM_ROWS, 1, WIDTH), F32),
@@ -431,7 +439,6 @@
         lax.fori_loop(0, count, body, 0)
 
     run(0, emb_blocks, (eg, ep, em, ev), emb_outs)
-    run(emb_blocks, mat_blocks, (mg, mp, mm, mv), mat_outs)
     new_p, new_m, new_v = adamw_block(ng[:NORM_ROWS, :NORM_COLS] * clip, np_[...], nm[...], nv[...], 0.0)
     for k, value in enumerate((new_p, new_m, new_v)):
         n_bufs[k] = value
@@ -440,6 +447,7 @@
     norm_copies.append(pltpu.make_async_copy(nb_buf, nb_out, n_sems.at[3]))
     for copy in norm_copies:
         copy.start()
+    run(emb_blocks, mat_blocks, (mg, mp, mm, mv), mat_outs)
     for slot in range(STORE_SLOTS):
         for copy in copies(emb_outs, slot, 0):
             copy.wait()

time: 270 us -> 268 us (level)
  no operation moved by 1% of the time
where the time goes in v9:
time: 268 us
  Pallas kernels  267 us (100%)
    pallas_call x1, Pallas kernels, reduce_grads(): pl.pallas_call(functools.partial(reduce_kernel, counts), out_shape=(jax.S...  257 us
    pallas_call x1, Pallas kernels, adamw(): pl.pallas_call(adamw_kernel, out_shape=tuple(shapes), in_specs=[vmem] * 1...  9.96 us

profile of v9, /device:TPU:0, one launch (start us, length us, event | category | flops | bytes accessed | tf_op | source)
XLA Modules:
  0.0 267.7 jit_solution(3131377850757182703)
XLA Ops:
  0.6 0.0 copy-start
  0.7 0.0 copy-start.1
  0.7 0.0 copy-start.2
  0.7 0.0 copy-start.3
  0.7 0.0 copy-start.4
  0.7 0.0 copy-start.5
  0.7 0.0 copy-start.6
  0.7 0.0 copy-start.7
  0.7 0.0 copy-start.8
  0.7 256.9 %reduce_grads.1 = (f32[256,5376]{1,0:T(8,128)S(1)}, f32[128,5376]{1,0:T(8,128)S(1)}, f32[16,768]{1,0:T(8,128)S(1)}, f32[8,128]{1,0:T(8,128)S(1)}) custom-call(f32[2,2,2,256,5376]{4,3,2,1,0:T(8,128)} %bitcast.3, f32[2,2,2,128,5376]{4,3,2,1,0:T(8,128)} %bitcast.4, f32[9,1,5376]{2,1,0:T(1,128)} %bitcast.5), custom_call_target="tpu_custom_call" | custom-call | tf_op jit(solution)/shard_map/reduce_grads/pallas_call | solution.py:368
  257.6 0.0 copy-done
  257.6 0.0 copy-done.1
  257.7 0.0 copy-done.2
  257.7 0.0 copy-done.3
  257.7 0.0 copy-done.4
  257.7 0.0 copy-done.5
  257.7 0.0 copy-done.6
  257.7 0.0 copy-done.7
  257.7 0.0 copy-done.8
  257.7 10.0 %adamw.1 = (f32[256,5376]{1,0:T(8,128)}, f32[256,5376]{1,0:T(8,128)}, f32[256,5376]{1,0:T(8,128)}, bf16[256,5376]{1,0:T(8,128)(2,1)}, f32[128,5376]{1,0:T(8,128)...) custom-call(f32[8,128]{1,0:T(8,128)S(1)} %get-tuple-element.16.scale, ...), custom_call_target="tpu_custom_call" | custom-call | flops 41287680 | bytes 61931520 | tf_op jit(solution)/shard_map/adamw/pallas_call | solution.py:466
Async XLA Ops:
  0.6 257.0 %copy-start = (f32[256,5376]{1,0:T(8,128)S(1)}, f32[256,5376]{1,0:T(8,128)}, u32[]{:S(2)}) copy-start(f32[256,5376]{1,0:T(8,128)} %ep.1) | copy-start | bytes 16515076
  0.7 257.0 %copy-start.1 = (f32[256,5376]{1,0:T(8,128)S(1)}, f32[256,5376]{1,0:T(8,128)}, u32[]{:S(2)}) copy-start(f32[256,5376]{1,0:T(8,128)} %em.1) | copy-start | bytes 16515076
  0.7 257.0 %copy-start.2 = (f32[256,5376]{1,0:T(8,128)S(1)}, f32[256,5376]{1,0:T(8,128)}, u32[]{:S(2)}) copy-start(f32[256,5376]{1,0:T(8,128)} %ev.1) | copy-start | bytes 16515076
  0.7 257.0 %copy-start.3 = (f32[128,5376]{1,0:T(8,128)S(1)}, f32[128,5376]{1,0:T(8,128)}, u32[]{:S(2)}) copy-start(f32[128,5376]{1,0:T(8,128)} %mp.1) | copy-start | bytes 8257540
  0.7 257.0 %copy-start.4 = (f32[128,5376]{1,0:T(8,128)S(1)}, f32[128,5376]{1,0:T(8,128)}, u32[]{:S(2)}) copy-start(f32[128,5376]{1,0:T(8,128)} %mm.1) | copy-start | bytes 8257540
  0.7 257.0 %copy-start.5 = (f32[128,5376]{1,0:T(8,128)S(1)}, f32[128,5376]{1,0:T(8,128)}, u32[]{:S(2)}) copy-start(f32[128,5376]{1,0:T(8,128)} %mv.1) | copy-start | bytes 8257540
  0.7 257.0 %copy-start.6 = (f32[9,672]{1,0:T(8,128)S(1)}, f32[9,672]{1,0:T(8,128)}, u32[]{:S(2)}) copy-start(f32[9,672]{1,0:T(8,128)} %np_.1) | copy-start | bytes 72580
  0.7 257.0 %copy-start.7 = (f32[9,672]{1,0:T(8,128)S(1)}, f32[9,672]{1,0:T(8,128)}, u32[]{:S(2)}) copy-start(f32[9,672]{1,0:T(8,128)} %nm.1) | copy-start | bytes 72580
  0.7 257.0 %copy-start.8 = (f32[9,672]{1,0:T(8,128)S(1)}, f32[9,672]{1,0:T(8,128)}, u32[]{:S(2)}) copy-start(f32[9,672]{1,0:T(8,128)} %nv.1) | copy-start | bytes 72580

commit v10 on v9

--- a/solution.py
+++ b/solution.py
@@ -26,6 +26,7 @@
 ROWS = 8
 PLANS = ((1920, 768), (2176, 512))
 INNER = (20, 44)
+CUT = 2 * min(side for side, _ in PLANS)
 SIDE_MAX = max(side for side, _ in PLANS)
 HALF_MAX = max(half for _, half in PLANS)
 LAG_ZERO = 1
@@ -86,9 +87,11 @@
         s = lax.rem(j, P_SLOTS)
         return pltpu.make_async_copy(ref.at[:, :, c, pl.ds(row, ROWS), :], part.at[s], load_sem.at[s])
 
-    def zero_copy(ref, row, j):
+    def zero_copies(ref, row, j):
         s = lax.rem(j, R_SLOTS)
-        return remote(ref.at[:, :, 1 - c, pl.ds(row, ROWS), :], recv_zero.at[s], zero_send.at[s], zero_recv.at[s], core)
+        return [remote(ref.at[:, :, 1 - c, pl.ds(row, ROWS), cols], recv_zero.at[s, :, :, :, cols],
+                       zero_send.at[k, s], zero_recv.at[k, s], core)
+                for k, cols in enumerate((pl.ds(CUT, WIDTH - CUT), pl.ds(0, CUT)))]
 
     def ones(j, side, half):
         s, r = lax.rem(j, P_SLOTS), lax.rem(j, RING)
@@ -154,27 +157,29 @@
 
         @pl.when(j >= R_SLOTS)
         def _():
-            zero_copy(emb, 0, j - R_SLOTS).wait_send()
+            wait_send(zero_copies(emb, 0, j - R_SLOTS))
             pl.semaphore_wait(credit, 1)
 
         def body(ref, _, row):
-            zero_copy(ref, row, j).start()
+            start(zero_copies(ref, row, j))
             load_copy(ref, row, j).start()
 
         on_rows(j, body)
 
     def stage_one(j):
         load_copy(emb, 0, j).wait()
-        zero_copy(emb, 0, j).wait_recv()
-        part[lax.rem(j, P_SLOTS)] += recv_zero[lax.rem(j, R_SLOTS)]
+        zero_copies(emb, 0, j)[0].wait_recv()
+        part[lax.rem(j, P_SLOTS), :, :, :, CUT:] += recv_zero[lax.rem(j, R_SLOTS), :, :, :, CUT:]
+        on_plan(j, lambda *args: start(ones(*args)[:1]))
+
+    def stage_one_more(j):
+        zero_copies(emb, 0, j)[1].wait_recv()
+        part[lax.rem(j, P_SLOTS), :, :, :, :CUT] += recv_zero[lax.rem(j, R_SLOTS), :, :, :, :CUT]
 
         @pl.when(j + R_SLOTS < total)
         def _():
             pl.semaphore_signal(credit, inc=1, device_id=core, device_id_type=MESH)
 
-        on_plan(j, lambda *args: start(ones(*args)[:1]))
-
-    def stage_one_more(j):
         on_plan(j, lambda *args: start(ones(*args)[1:]))
 
     def stage_two(j):
@@ -315,7 +320,7 @@
         lax.fori_loop(total - slots, total, body, 0)
 
     drain(P_SLOTS, ones)
-    drain(R_SLOTS, lambda j, side, half: (zero_copy(emb, 0, j),))
+    drain(R_SLOTS, lambda j, side, half: zero_copies(emb, 0, j))
     drain(SEND_SLOTS, lambda *args: twos(*args) + (two_c_even(*args), three_ab(*args), three_c(*args), four(*args, z)))
 
     def last(j, carry):
@@ -358,7 +363,7 @@
         pltpu.VMEM(NORM_PAD, F32),
         pltpu.VMEM((8, 128), F32),
         pltpu.VMEM((8, 8, 128), F32),
-        dma((P_SLOTS,)), dma((R_SLOTS,)), dma((R_SLOTS,)), pltpu.SemaphoreType.REGULAR,
+        dma((P_SLOTS,)), dma((2, R_SLOTS)), dma((2, R_SLOTS)), pltpu.SemaphoreType.REGULAR,
         dma((3, P_SLOTS)), dma((3, RING)), dma((3, SEND_SLOTS)), dma((3, RING)),
         dma((2, SEND_SLOTS)), dma((2, RING)), dma((SEND_SLOTS,)), dma((RING,)), dma((SEND_SLOTS,)),
         dma, dma((4,)), dma((4,)), dma((7,)), dma((8,)),
@@ -387,6 +392,7 @@
 
 BLOCK = 16
 COLS = 384
+SIDE = WIDTH // 2
 STORE_SLOTS = 4
 
 
@@ -404,8 +410,9 @@
                  p_buf, m_buf, v_buf, b_buf, n_bufs, nb_buf, sems, n_sems):
     clip = scale[0:1, 0:1]
 
-    def copies(outs, slot, row):
-        return [pltpu.make_async_copy(buf.at[slot], out.at[pl.ds(row, BLOCK), :], sems.at[k, slot])
+    def copies(outs, slot, row, side):
+        cols = pl.ds(side * SIDE, SIDE)
+        return [pltpu.make_async_copy(buf.at[slot, side], out.at[pl.ds(row, BLOCK), cols], sems.at[k, slot, side])
                 for k, (buf, out) in enumerate(zip((p_buf, m_buf, v_buf, b_buf), outs))]
 
     emb_outs = (ep_out, em_out, ev_out, eb_out)
@@ -418,27 +425,29 @@
             j = first + i
             slot = lax.rem(j, STORE_SLOTS)
 
-            @pl.when(j >= STORE_SLOTS)
-            def _():
-                for copy in copies(emb_outs, slot, 0):
-                    copy.wait()
-
             row = pl.multiple_of(i * BLOCK, BLOCK)
-            for col in range(0, WIDTH, COLS):
-                cols = pl.ds(col, COLS)
-                g, p, m, v = (ref[pl.ds(row, BLOCK), cols] for ref in ins)
-                new_p, new_m, new_v = adamw_block(g * clip, p, m, v, WEIGHT_DECAY)
-                p_buf[slot, :, cols] = new_p
-                m_buf[slot, :, cols] = new_m
-                v_buf[slot, :, cols] = new_v
-                b_buf[slot, :, cols] = new_p.astype(jnp.bfloat16)
-            for copy in copies(outs, slot, row):
-                copy.start()
+            for side in range(2):
+                @pl.when(j >= STORE_SLOTS)
+                def _():
+                    for copy in copies(emb_outs, slot, 0, side):
+                        copy.wait()
+
+                for col in range(0, SIDE, COLS):
+                    here, cols = pl.ds(col, COLS), pl.ds(side * SIDE + col, COLS)
+                    g, p, m, v = (ref[pl.ds(row, BLOCK), cols] for ref in ins)
+                    new_p, new_m, new_v = adamw_block(g * clip, p, m, v, WEIGHT_DECAY)
+                    p_buf[slot, side, :, here] = new_p
+                    m_buf[slot, side, :, here] = new_m
+                    v_buf[slot, side, :, here] = new_v
+                    b_buf[slot, side, :, here] = new_p.astype(jnp.bfloat16)
+                for copy in copies(outs, slot, row, side):
+                    copy.start()
             return carry
 
         lax.fori_loop(0, count, body, 0)
 
     run(0, emb_blocks, (eg, ep, em, ev), emb_outs)
+    run(emb_blocks, mat_blocks, (mg, mp, mm, mv), mat_outs)
     new_p, new_m, new_v = adamw_block(ng[:NORM_ROWS, :NORM_COLS] * clip, np_[...], nm[...], nv[...], 0.0)
     for k, value in enumerate((new_p, new_m, new_v)):
         n_bufs[k] = value
@@ -447,10 +456,10 @@
     norm_copies.append(pltpu.make_async_copy(nb_buf, nb_out, n_sems.at[3]))
     for copy in norm_copies:
         copy.start()
-    run(emb_blocks, mat_blocks, (mg, mp, mm, mv), mat_outs)
     for slot in range(STORE_SLOTS):
-        for copy in copies(emb_outs, slot, 0):
-            copy.wait()
+        for side in range(2):
+            for copy in copies(emb_outs, slot, 0, side):
+                copy.wait()
     for copy in norm_copies:
         copy.wait()
 
@@ -459,7 +468,7 @@
     shapes = []
     for ref in (emb[1], mat[1], norm[1]):
         shapes += [jax.ShapeDtypeStruct(ref.shape, F32)] * 3 + [jax.ShapeDtypeStruct(ref.shape, jnp.bfloat16)]
-    buf = (STORE_SLOTS, BLOCK, WIDTH)
+    buf = (STORE_SLOTS, 2, BLOCK, SIDE)
     vmem = pl.BlockSpec(memory_space=pltpu.VMEM)
     hbm = pl.BlockSpec(memory_space=pl.ANY)
     elements = emb[1].size + mat[1].size
@@ -471,7 +480,7 @@
         scratch_shapes=[
             pltpu.VMEM(buf, F32), pltpu.VMEM(buf, F32), pltpu.VMEM(buf, F32), pltpu.VMEM(buf, jnp.bfloat16),
             pltpu.VMEM((3, NORM_ROWS, NORM_COLS), F32), pltpu.VMEM((NORM_ROWS, NORM_COLS), jnp.bfloat16),
-            pltpu.SemaphoreType.DMA((4, STORE_SLOTS)), pltpu.SemaphoreType.DMA((4,)),
+            pltpu.SemaphoreType.DMA((4, STORE_SLOTS, 2)), pltpu.SemaphoreType.DMA((4,)),
         ],
         compiler_params=pltpu.CompilerParams(vmem_limit_bytes=8 * 1024 * 1024),
         cost_estimate=pl.CostEstimate(flops=20 * elements, bytes_accessed=30 * elements, transcendentals=2 * elements),

time: 268 us -> 268 us (level)
  no operation moved by 1% of the time
where the time goes in v10:
time: 268 us
  Pallas kernels  267 us (100%)
    pallas_call x1, Pallas kernels, reduce_grads(): pl.pallas_call(functools.partial(reduce_kernel, counts), out_shape=(jax.S...  257 us
    pallas_call x1, Pallas kernels, adamw(): pl.pallas_call(adamw_kernel, out_shape=tuple(shapes), in_specs=[vmem] * 1...  9.95 us

profile of v10, /device:TPU:0, one launch (start us, length us, event | category | flops | bytes accessed | tf_op | source)
XLA Modules:
  0.0 267.6 jit_solution(12480447007344836647)
XLA Ops:
  0.6 0.0 copy-start
  0.7 0.0 copy-start.1
  0.7 0.0 copy-start.2
  0.7 0.0 copy-start.3
  0.7 0.0 copy-start.4
  0.7 0.0 copy-start.5
  0.7 0.0 copy-start.6
  0.7 0.0 copy-start.7
  0.7 0.0 copy-start.8
  0.7 256.9 %reduce_grads.1 = (f32[256,5376]{1,0:T(8,128)S(1)}, f32[128,5376]{1,0:T(8,128)S(1)}, f32[16,768]{1,0:T(8,128)S(1)}, f32[8,128]{1,0:T(8,128)S(1)}) custom-call(f32[2,2,2,256,5376]{4,3,2,1,0:T(8,128)} %bitcast.3, f32[2,2,2,128,5376]{4,3,2,1,0:T(8,128)} %bitcast.4, f32[9,1,5376]{2,1,0:T(1,128)} %bitcast.5), custom_call_target="tpu_custom_call" | custom-call | tf_op jit(solution)/shard_map/reduce_grads/pallas_call | solution.py:373
  257.6 0.0 copy-done
  257.6 0.0 copy-done.1
  257.6 0.0 copy-done.2
  257.6 0.0 copy-done.3
  257.6 0.0 copy-done.4
  257.7 0.0 copy-done.5
  257.7 0.0 copy-done.6
  257.7 0.0 copy-done.7
  257.7 0.0 copy-done.8
  257.7 9.9 %adamw.1 = (f32[256,5376]{1,0:T(8,128)}, f32[256,5376]{1,0:T(8,128)}, f32[256,5376]{1,0:T(8,128)}, bf16[256,5376]{1,0:T(8,128)(2,1)}, f32[128,5376]{1,0:T(8,128)...) custom-call(f32[8,128]{1,0:T(8,128)S(1)} %get-tuple-element.16.scale, ...), custom_call_target="tpu_custom_call" | custom-call | flops 41287680 | bytes 61931520 | tf_op jit(solution)/shard_map/adamw/pallas_call | solution.py:475
Async XLA Ops:
  0.6 257.0 %copy-start = (f32[256,5376]{1,0:T(8,128)S(1)}, f32[256,5376]{1,0:T(8,128)}, u32[]{:S(2)}) copy-start(f32[256,5376]{1,0:T(8,128)} %ep.1) | copy-start | bytes 16515076
  0.7 257.0 %copy-start.1 = (f32[256,5376]{1,0:T(8,128)S(1)}, f32[256,5376]{1,0:T(8,128)}, u32[]{:S(2)}) copy-start(f32[256,5376]{1,0:T(8,128)} %em.1) | copy-start | bytes 16515076
  0.7 257.0 %copy-start.2 = (f32[256,5376]{1,0:T(8,128)S(1)}, f32[256,5376]{1,0:T(8,128)}, u32[]{:S(2)}) copy-start(f32[256,5376]{1,0:T(8,128)} %ev.1) | copy-start | bytes 16515076
  0.7 257.0 %copy-start.3 = (f32[128,5376]{1,0:T(8,128)S(1)}, f32[128,5376]{1,0:T(8,128)}, u32[]{:S(2)}) copy-start(f32[128,5376]{1,0:T(8,128)} %mp.1) | copy-start | bytes 8257540
  0.7 257.0 %copy-start.4 = (f32[128,5376]{1,0:T(8,128)S(1)}, f32[128,5376]{1,0:T(8,128)}, u32[]{:S(2)}) copy-start(f32[128,5376]{1,0:T(8,128)} %mm.1) | copy-start | bytes 8257540
  0.7 257.0 %copy-start.5 = (f32[128,5376]{1,0:T(8,128)S(1)}, f32[128,5376]{1,0:T(8,128)}, u32[]{:S(2)}) copy-start(f32[128,5376]{1,0:T(8,128)} %mv.1) | copy-start | bytes 8257540
  0.7 257.0 %copy-start.6 = (f32[9,672]{1,0:T(8,128)S(1)}, f32[9,672]{1,0:T(8,128)}, u32[]{:S(2)}) copy-start(f32[9,672]{1,0:T(8,128)} %np_.1) | copy-start | bytes 72580
  0.7 257.0 %copy-start.7 = (f32[9,672]{1,0:T(8,128)S(1)}, f32[9,672]{1,0:T(8,128)}, u32[]{:S(2)}) copy-start(f32[9,672]{1,0:T(8,128)} %nm.1) | copy-start | bytes 72580
  0.7 257.0 %copy-start.8 = (f32[9,672]{1,0:T(8,128)S(1)}, f32[9,672]{1,0:T(8,128)}, u32[]{:S(2)}) copy-start(f32[9,672]{1,0:T(8,128)} %nv.1) | copy-start | bytes 72580

commit v11 on v10

--- a/solution.py
+++ b/solution.py
@@ -29,7 +29,7 @@
 CUT = 2 * min(side for side, _ in PLANS)
 SIDE_MAX = max(side for side, _ in PLANS)
 HALF_MAX = max(half for _, half in PLANS)
-LAG_ZERO = 1
+LAG_ZERO = 0
 LAG = 2
 P_SLOTS = 10
 R_SLOTS = 6
@@ -87,11 +87,12 @@
         s = lax.rem(j, P_SLOTS)
         return pltpu.make_async_copy(ref.at[:, :, c, pl.ds(row, ROWS), :], part.at[s], load_sem.at[s])
 
+    def exchange(source, s):
+        return [remote(source.at[:, :, :, cols], recv_zero.at[s, :, :, :, cols], zero_send.at[k, s], zero_recv.at[k, s], core)
+                for k, cols in enumerate((pl.ds(CUT, WIDTH - CUT), pl.ds(0, CUT)))]
+
     def zero_copies(ref, row, j):
-        s = lax.rem(j, R_SLOTS)
-        return [remote(ref.at[:, :, 1 - c, pl.ds(row, ROWS), cols], recv_zero.at[s, :, :, :, cols],
-                       zero_send.at[k, s], zero_recv.at[k, s], core)
-                for k, cols in enumerate((pl.ds(CUT, WIDTH - CUT), pl.ds(0, CUT)))]
+        return exchange(ref.at[:, :, 1 - c, pl.ds(row, ROWS)], lax.rem(j, R_SLOTS))
 
     def ones(j, side, half):
         s, r = lax.rem(j, P_SLOTS), lax.rem(j, RING)
@@ -257,7 +258,7 @@
         on_rows(j, store)
 
     def trip(it, carry):
-        when_in(it, stage_issue)
+        when_in(it + 1, stage_issue)
         when_in(it - LAG_ZERO, stage_one)
         when_in(it - LAG_ZERO - 4 * LAG, stage_five)
         when_in(it - LAG_ZERO - 3 * LAG, stage_four)
@@ -301,9 +302,14 @@
 
         return carry
 
+    ahead = pltpu.make_async_copy(emb.at[:, :, 1 - c, pl.ds(0, ROWS), :], part.at[P_SLOTS - 1], load_sem.at[P_SLOTS - 1])
+    ahead.start()
+    load_copy(emb, 0, 0).start()
     norm_part[...] = jnp.zeros_like(norm_part)
     square[...] = jnp.zeros_like(square)
+    ahead.wait()
     pl.semaphore_wait(barrier, 4)
+    start(exchange(part.at[P_SLOTS - 1], 0))
     lax.fori_loop(0, total + LAG_ZERO + 4 * LAG, trip, 0)
 
     value = jnp.full((8, 128), jnp.sum(square[...]), F32)

time: 268 us -> 268 us (level)
  no operation moved by 1% of the time
where the time goes in v11:
time: 268 us
  Pallas kernels  267 us (100%)
    pallas_call x1, Pallas kernels, reduce_grads(): pl.pallas_call(functools.partial(reduce_kernel, counts), out_shape=(jax.S...  257 us
    pallas_call x1, Pallas kernels, adamw(): pl.pallas_call(adamw_kernel, out_shape=tuple(shapes), in_specs=[vmem] * 1...  9.95 us

profile of v11, /device:TPU:0, one launch (start us, length us, event | category | flops | bytes accessed | tf_op | source)
XLA Modules:
  0.0 267.6 jit_solution(2192171130068578112)
XLA Ops:
  0.6 0.0 copy-start
  0.7 0.0 copy-start.1
  0.7 0.0 copy-start.2
  0.7 0.0 copy-start.3
  0.7 0.0 copy-start.4
  0.7 0.0 copy-start.5
  0.7 0.0 copy-start.6
  0.7 0.0 copy-start.7
  0.7 0.0 copy-start.8
  0.7 256.8 %reduce_grads.1 = (f32[256,5376]{1,0:T(8,128)S(1)}, f32[128,5376]{1,0:T(8,128)S(1)}, f32[16,768]{1,0:T(8,128)S(1)}, f32[8,128]{1,0:T(8,128)S(1)}) custom-call(f32[2,2,2,256,5376]{4,3,2,1,0:T(8,128)} %bitcast.3, f32[2,2,2,128,5376]{4,3,2,1,0:T(8,128)} %bitcast.4, f32[9,1,5376]{2,1,0:T(1,128)} %bitcast.5), custom_call_target="tpu_custom_call" | custom-call | tf_op jit(solution)/shard_map/reduce_grads/pallas_call | solution.py:379
  257.5 0.0 copy-done
  257.6 0.0 copy-done.1
  257.6 0.0 copy-done.2
  257.6 0.0 copy-done.3
  257.6 0.0 copy-done.4
  257.6 0.0 copy-done.5
  257.6 0.0 copy-done.6
  257.6 0.0 copy-done.7
  257.6 0.0 copy-done.8
  257.6 9.9 %adamw.1 = (f32[256,5376]{1,0:T(8,128)}, f32[256,5376]{1,0:T(8,128)}, f32[256,5376]{1,0:T(8,128)}, bf16[256,5376]{1,0:T(8,128)(2,1)}, f32[128,5376]{1,0:T(8,128)...) custom-call(f32[8,128]{1,0:T(8,128)S(1)} %get-tuple-element.16.scale, ...), custom_call_target="tpu_custom_call" | custom-call | flops 41287680 | bytes 61931520 | tf_op jit(solution)/shard_map/adamw/pallas_call | solution.py:481
Async XLA Ops:
  0.6 256.9 %copy-start = (f32[256,5376]{1,0:T(8,128)S(1)}, f32[256,5376]{1,0:T(8,128)}, u32[]{:S(2)}) copy-start(f32[256,5376]{1,0:T(8,128)} %ep.1) | copy-start | bytes 16515076
  0.7 256.9 %copy-start.1 = (f32[256,5376]{1,0:T(8,128)S(1)}, f32[256,5376]{1,0:T(8,128)}, u32[]{:S(2)}) copy-start(f32[256,5376]{1,0:T(8,128)} %em.1) | copy-start | bytes 16515076
  0.7 256.9 %copy-start.2 = (f32[256,5376]{1,0:T(8,128)S(1)}, f32[256,5376]{1,0:T(8,128)}, u32[]{:S(2)}) copy-start(f32[256,5376]{1,0:T(8,128)} %ev.1) | copy-start | bytes 16515076
  0.7 256.9 %copy-start.3 = (f32[128,5376]{1,0:T(8,128)S(1)}, f32[128,5376]{1,0:T(8,128)}, u32[]{:S(2)}) copy-start(f32[128,5376]{1,0:T(8,128)} %mp.1) | copy-start | bytes 8257540
  0.7 256.9 %copy-start.4 = (f32[128,5376]{1,0:T(8,128)S(1)}, f32[128,5376]{1,0:T(8,128)}, u32[]{:S(2)}) copy-start(f32[128,5376]{1,0:T(8,128)} %mm.1) | copy-start | bytes 8257540
  0.7 256.9 %copy-start.5 = (f32[128,5376]{1,0:T(8,128)S(1)}, f32[128,5376]{1,0:T(8,128)}, u32[]{:S(2)}) copy-start(f32[128,5376]{1,0:T(8,128)} %mv.1) | copy-start | bytes 8257540
  0.7 256.9 %copy-start.6 = (f32[9,672]{1,0:T(8,128)S(1)}, f32[9,672]{1,0:T(8,128)}, u32[]{:S(2)}) copy-start(f32[9,672]{1,0:T(8,128)} %np_.1) | copy-start | bytes 72580
  0.7 256.9 %copy-start.7 = (f32[9,672]{1,0:T(8,128)S(1)}, f32[9,672]{1,0:T(8,128)}, u32[]{:S(2)}) copy-start(f32[9,672]{1,0:T(8,128)} %nm.1) | copy-start | bytes 72580
  0.7 256.9 %copy-start.8 = (f32[9,672]{1,0:T(8,128)S(1)}, f32[9,672]{1,0:T(8,128)}, u32[]{:S(2)}) copy-start(f32[9,672]{1,0:T(8,128)} %nv.1) | copy-start | bytes 72580

commit v12 on v11

--- a/solution.py
+++ b/solution.py
@@ -25,7 +25,7 @@
 NORM_PAD = (16, 768)
 ROWS = 8
 PLANS = ((1920, 768), (2176, 512))
-INNER = (20, 44)
+INNER = (24, 44)
 CUT = 2 * min(side for side, _ in PLANS)
 SIDE_MAX = max(side for side, _ in PLANS)
 HALF_MAX = max(half for _, half in PLANS)

time: 268 us -> 268 us (level)
  no operation moved by 1% of the time
where the time goes in v12:
time: 268 us
  Pallas kernels  267 us (100%)
    pallas_call x1, Pallas kernels, reduce_grads(): pl.pallas_call(functools.partial(reduce_kernel, counts), out_shape=(jax.S...  257 us
    pallas_call x1, Pallas kernels, adamw(): pl.pallas_call(adamw_kernel, out_shape=tuple(shapes), in_specs=[vmem] * 1...  9.95 us

profile of v12, /device:TPU:0, one launch (start us, length us, event | category | flops | bytes accessed | tf_op | source)
XLA Modules:
  0.0 268.2 jit_solution(13443122277758504354)
XLA Ops:
  0.6 0.0 copy-start
  0.7 0.0 copy-start.1
  0.7 0.0 copy-start.2
  0.7 0.0 copy-start.3
  0.7 0.0 copy-start.4
  0.7 0.0 copy-start.5
  0.7 0.0 copy-start.6
  0.7 0.0 copy-start.7
  0.7 0.0 copy-start.8
  0.7 257.4 %reduce_grads.1 = (f32[256,5376]{1,0:T(8,128)S(1)}, f32[128,5376]{1,0:T(8,128)S(1)}, f32[16,768]{1,0:T(8,128)S(1)}, f32[8,128]{1,0:T(8,128)S(1)}) custom-call(f32[2,2,2,256,5376]{4,3,2,1,0:T(8,128)} %bitcast.3, f32[2,2,2,128,5376]{4,3,2,1,0:T(8,128)} %bitcast.4, f32[9,1,5376]{2,1,0:T(1,128)} %bitcast.5), custom_call_target="tpu_custom_call" | custom-call | tf_op jit(solution)/shard_map/reduce_grads/pallas_call | solution.py:379
  258.2 0.0 copy-done
  258.2 0.0 copy-done.1
  258.2 0.0 copy-done.2
  258.2 0.0 copy-done.3
  258.2 0.0 copy-done.4
  258.2 0.0 copy-done.5
  258.2 0.0 copy-done.6
  258.2 0.0 copy-done.7
  258.2 0.0 copy-done.8
  258.3 9.9 %adamw.1 = (f32[256,5376]{1,0:T(8,128)}, f32[256,5376]{1,0:T(8,128)}, f32[256,5376]{1,0:T(8,128)}, bf16[256,5376]{1,0:T(8,128)(2,1)}, f32[128,5376]{1,0:T(8,128)...) custom-call(f32[8,128]{1,0:T(8,128)S(1)} %get-tuple-element.16.scale, ...), custom_call_target="tpu_custom_call" | custom-call | flops 41287680 | bytes 61931520 | tf_op jit(solution)/shard_map/adamw/pallas_call | solution.py:481
Async XLA Ops:
  0.6 257.5 %copy-start = (f32[256,5376]{1,0:T(8,128)S(1)}, f32[256,5376]{1,0:T(8,128)}, u32[]{:S(2)}) copy-start(f32[256,5376]{1,0:T(8,128)} %ep.1) | copy-start | bytes 16515076
  0.7 257.5 %copy-start.1 = (f32[256,5376]{1,0:T(8,128)S(1)}, f32[256,5376]{1,0:T(8,128)}, u32[]{:S(2)}) copy-start(f32[256,5376]{1,0:T(8,128)} %em.1) | copy-start | bytes 16515076
  0.7 257.5 %copy-start.2 = (f32[256,5376]{1,0:T(8,128)S(1)}, f32[256,5376]{1,0:T(8,128)}, u32[]{:S(2)}) copy-start(f32[256,5376]{1,0:T(8,128)} %ev.1) | copy-start | bytes 16515076
  0.7 257.5 %copy-start.3 = (f32[128,5376]{1,0:T(8,128)S(1)}, f32[128,5376]{1,0:T(8,128)}, u32[]{:S(2)}) copy-start(f32[128,5376]{1,0:T(8,128)} %mp.1) | copy-start | bytes 8257540
  0.7 257.5 %copy-start.4 = (f32[128,5376]{1,0:T(8,128)S(1)}, f32[128,5376]{1,0:T(8,128)}, u32[]{:S(2)}) copy-start(f32[128,5376]{1,0:T(8,128)} %mm.1) | copy-start | bytes 8257540
  0.7 257.5 %copy-start.5 = (f32[128,5376]{1,0:T(8,128)S(1)}, f32[128,5376]{1,0:T(8,128)}, u32[]{:S(2)}) copy-start(f32[128,5376]{1,0:T(8,128)} %mv.1) | copy-start | bytes 8257540
  0.7 257.5 %copy-start.6 = (f32[9,672]{1,0:T(8,128)S(1)}, f32[9,672]{1,0:T(8,128)}, u32[]{:S(2)}) copy-start(f32[9,672]{1,0:T(8,128)} %np_.1) | copy-start | bytes 72580
  0.7 257.5 %copy-start.7 = (f32[9,672]{1,0:T(8,128)S(1)}, f32[9,672]{1,0:T(8,128)}, u32[]{:S(2)}) copy-start(f32[9,672]{1,0:T(8,128)} %nm.1) | copy-start | bytes 72580
  0.7 257.5 %copy-start.8 = (f32[9,672]{1,0:T(8,128)S(1)}, f32[9,672]{1,0:T(8,128)}, u32[]{:S(2)}) copy-start(f32[9,672]{1,0:T(8,128)} %nv.1) | copy-start | bytes 72580

commit v13 on v12

--- a/solution.py
+++ b/solution.py
@@ -24,8 +24,8 @@
 NORM_COLS = 672
 NORM_PAD = (16, 768)
 ROWS = 8
-PLANS = ((1920, 768), (2176, 512))
-INNER = (24, 44)
+PLANS = ((1792, 896), (2176, 512))
+INNER = (14, 46)
 CUT = 2 * min(side for side, _ in PLANS)
 SIDE_MAX = max(side for side, _ in PLANS)
 HALF_MAX = max(half for _, half in PLANS)

time: 268 us -> 267 us (level)
  no operation moved by 1% of the time
where the time goes in v13:
time: 267 us
  Pallas kernels  267 us (100%)
    pallas_call x1, Pallas kernels, reduce_grads(): pl.pallas_call(functools.partial(reduce_kernel, counts), out_shape=(jax.S...  257 us
    pallas_call x1, Pallas kernels, adamw(): pl.pallas_call(adamw_kernel, out_shape=tuple(shapes), in_specs=[vmem] * 1...  9.95 us

profile of v13, /device:TPU:0, one launch (start us, length us, event | category | flops | bytes accessed | tf_op | source)
XLA Modules:
  0.0 267.4 jit_solution(17271764431257529926)
XLA Ops:
  0.6 0.0 copy-start
  0.7 0.0 copy-start.1
  0.7 0.0 copy-start.2
  0.7 0.0 copy-start.3
  0.7 0.0 copy-start.4
  0.7 0.0 copy-start.5
  0.7 0.0 copy-start.6
  0.7 0.0 copy-start.7
  0.7 0.0 copy-start.8
  0.7 256.6 %reduce_grads.1 = (f32[256,5376]{1,0:T(8,128)S(1)}, f32[128,5376]{1,0:T(8,128)S(1)}, f32[16,768]{1,0:T(8,128)S(1)}, f32[8,128]{1,0:T(8,128)S(1)}) custom-call(f32[2,2,2,256,5376]{4,3,2,1,0:T(8,128)} %bitcast.3, f32[2,2,2,128,5376]{4,3,2,1,0:T(8,128)} %bitcast.4, f32[9,1,5376]{2,1,0:T(1,128)} %bitcast.5), custom_call_target="tpu_custom_call" | custom-call | tf_op jit(solution)/shard_map/reduce_grads/pallas_call | solution.py:379
  257.3 0.0 copy-done
  257.3 0.0 copy-done.1
  257.3 0.0 copy-done.2
  257.4 0.0 copy-done.3
  257.4 0.0 copy-done.4
  257.4 0.0 copy-done.5
  257.4 0.0 copy-done.6
  257.4 0.0 copy-done.7
  257.4 0.0 copy-done.8
  257.4 9.9 %adamw.1 = (f32[256,5376]{1,0:T(8,128)}, f32[256,5376]{1,0:T(8,128)}, f32[256,5376]{1,0:T(8,128)}, bf16[256,5376]{1,0:T(8,128)(2,1)}, f32[128,5376]{1,0:T(8,128)...) custom-call(f32[8,128]{1,0:T(8,128)S(1)} %get-tuple-element.16.scale, ...), custom_call_target="tpu_custom_call" | custom-call | flops 41287680 | bytes 61931520 | tf_op jit(solution)/shard_map/adamw/pallas_call | solution.py:481
Async XLA Ops:
  0.6 256.7 %copy-start = (f32[256,5376]{1,0:T(8,128)S(1)}, f32[256,5376]{1,0:T(8,128)}, u32[]{:S(2)}) copy-start(f32[256,5376]{1,0:T(8,128)} %ep.1) | copy-start | bytes 16515076
  0.7 256.7 %copy-start.1 = (f32[256,5376]{1,0:T(8,128)S(1)}, f32[256,5376]{1,0:T(8,128)}, u32[]{:S(2)}) copy-start(f32[256,5376]{1,0:T(8,128)} %em.1) | copy-start | bytes 16515076
  0.7 256.7 %copy-start.2 = (f32[256,5376]{1,0:T(8,128)S(1)}, f32[256,5376]{1,0:T(8,128)}, u32[]{:S(2)}) copy-start(f32[256,5376]{1,0:T(8,128)} %ev.1) | copy-start | bytes 16515076
  0.7 256.7 %copy-start.3 = (f32[128,5376]{1,0:T(8,128)S(1)}, f32[128,5376]{1,0:T(8,128)}, u32[]{:S(2)}) copy-start(f32[128,5376]{1,0:T(8,128)} %mp.1) | copy-start | bytes 8257540
  0.7 256.7 %copy-start.4 = (f32[128,5376]{1,0:T(8,128)S(1)}, f32[128,5376]{1,0:T(8,128)}, u32[]{:S(2)}) copy-start(f32[128,5376]{1,0:T(8,128)} %mm.1) | copy-start | bytes 8257540
  0.7 256.7 %copy-start.5 = (f32[128,5376]{1,0:T(8,128)S(1)}, f32[128,5376]{1,0:T(8,128)}, u32[]{:S(2)}) copy-start(f32[128,5376]{1,0:T(8,128)} %mv.1) | copy-start | bytes 8257540
  0.7 256.7 %copy-start.6 = (f32[9,672]{1,0:T(8,128)S(1)}, f32[9,672]{1,0:T(8,128)}, u32[]{:S(2)}) copy-start(f32[9,672]{1,0:T(8,128)} %np_.1) | copy-start | bytes 72580
  0.7 256.7 %copy-start.7 = (f32[9,672]{1,0:T(8,128)S(1)}, f32[9,672]{1,0:T(8,128)}, u32[]{:S(2)}) copy-start(f32[9,672]{1,0:T(8,128)} %nm.1) | copy-start | bytes 72580
  0.7 256.7 %copy-start.8 = (f32[9,672]{1,0:T(8,128)S(1)}, f32[9,672]{1,0:T(8,128)}, u32[]{:S(2)}) copy-start(f32[9,672]{1,0:T(8,128)} %nv.1) | copy-start | bytes 72580

commit v14 on v13

--- a/solution.py
+++ b/solution.py
@@ -25,7 +25,7 @@
 NORM_PAD = (16, 768)
 ROWS = 8
 PLANS = ((1792, 896), (2176, 512))
-INNER = (14, 46)
+INNER = (12, 44)
 CUT = 2 * min(side for side, _ in PLANS)
 SIDE_MAX = max(side for side, _ in PLANS)
 HALF_MAX = max(half for _, half in PLANS)
@@ -307,8 +307,8 @@
     load_copy(emb, 0, 0).start()
     norm_part[...] = jnp.zeros_like(norm_part)
     square[...] = jnp.zeros_like(square)
+    pl.semaphore_wait(barrier, 4)
     ahead.wait()
-    pl.semaphore_wait(barrier, 4)
     start(exchange(part.at[P_SLOTS - 1], 0))
     lax.fori_loop(0, total + LAG_ZERO + 4 * LAG, trip, 0)
 

time: 267 us -> 267 us (level)
  no operation moved by 1% of the time
where the time goes in v14:
time: 267 us
  Pallas kernels  267 us (100%)
    pallas_call x1, Pallas kernels, reduce_grads(): pl.pallas_call(functools.partial(reduce_kernel, counts), out_shape=(jax.S...  257 us
    pallas_call x1, Pallas kernels, adamw(): pl.pallas_call(adamw_kernel, out_shape=tuple(shapes), in_specs=[vmem] * 1...  9.95 us

profile of v14, /device:TPU:0, one launch (start us, length us, event | category | flops | bytes accessed | tf_op | source)
XLA Modules:
  0.0 267.4 jit_solution(15766488357288493901)
XLA Ops:
  0.6 0.0 copy-start
  0.7 0.0 copy-start.1
  0.7 0.0 copy-start.2
  0.7 0.0 copy-start.3
  0.7 0.0 copy-start.4
  0.7 0.0 copy-start.5
  0.7 0.0 copy-start.6
  0.7 0.0 copy-start.7
  0.7 0.0 copy-start.8
  0.7 256.6 %reduce_grads.1 = (f32[256,5376]{1,0:T(8,128)S(1)}, f32[128,5376]{1,0:T(8,128)S(1)}, f32[16,768]{1,0:T(8,128)S(1)}, f32[8,128]{1,0:T(8,128)S(1)}) custom-call(f32[2,2,2,256,5376]{4,3,2,1,0:T(8,128)} %bitcast.3, f32[2,2,2,128,5376]{4,3,2,1,0:T(8,128)} %bitcast.4, f32[9,1,5376]{2,1,0:T(1,128)} %bitcast.5), custom_call_target="tpu_custom_call" | custom-call | tf_op jit(solution)/shard_map/reduce_grads/pallas_call | solution.py:379
  257.3 0.0 copy-done
  257.3 0.0 copy-done.1
  257.3 0.0 copy-done.2
  257.4 0.0 copy-done.3
  257.4 0.0 copy-done.4
  257.4 0.0 copy-done.5
  257.4 0.0 copy-done.6
  257.4 0.0 copy-done.7
  257.4 0.0 copy-done.8
  257.4 9.9 %adamw.1 = (f32[256,5376]{1,0:T(8,128)}, f32[256,5376]{1,0:T(8,128)}, f32[256,5376]{1,0:T(8,128)}, bf16[256,5376]{1,0:T(8,128)(2,1)}, f32[128,5376]{1,0:T(8,128)...) custom-call(f32[8,128]{1,0:T(8,128)S(1)} %get-tuple-element.16.scale, ...), custom_call_target="tpu_custom_call" | custom-call | flops 41287680 | bytes 61931520 | tf_op jit(solution)/shard_map/adamw/pallas_call | solution.py:481
Async XLA Ops:
  0.6 256.7 %copy-start = (f32[256,5376]{1,0:T(8,128)S(1)}, f32[256,5376]{1,0:T(8,128)}, u32[]{:S(2)}) copy-start(f32[256,5376]{1,0:T(8,128)} %ep.1) | copy-start | bytes 16515076
  0.7 256.7 %copy-start.1 = (f32[256,5376]{1,0:T(8,128)S(1)}, f32[256,5376]{1,0:T(8,128)}, u32[]{:S(2)}) copy-start(f32[256,5376]{1,0:T(8,128)} %em.1) | copy-start | bytes 16515076
  0.7 256.7 %copy-start.2 = (f32[256,5376]{1,0:T(8,128)S(1)}, f32[256,5376]{1,0:T(8,128)}, u32[]{:S(2)}) copy-start(f32[256,5376]{1,0:T(8,128)} %ev.1) | copy-start | bytes 16515076
  0.7 256.7 %copy-start.3 = (f32[128,5376]{1,0:T(8,128)S(1)}, f32[128,5376]{1,0:T(8,128)}, u32[]{:S(2)}) copy-start(f32[128,5376]{1,0:T(8,128)} %mp.1) | copy-start | bytes 8257540
  0.7 256.7 %copy-start.4 = (f32[128,5376]{1,0:T(8,128)S(1)}, f32[128,5376]{1,0:T(8,128)}, u32[]{:S(2)}) copy-start(f32[128,5376]{1,0:T(8,128)} %mm.1) | copy-start | bytes 8257540
  0.7 256.7 %copy-start.5 = (f32[128,5376]{1,0:T(8,128)S(1)}, f32[128,5376]{1,0:T(8,128)}, u32[]{:S(2)}) copy-start(f32[128,5376]{1,0:T(8,128)} %mv.1) | copy-start | bytes 8257540
  0.7 256.7 %copy-start.6 = (f32[9,672]{1,0:T(8,128)S(1)}, f32[9,672]{1,0:T(8,128)}, u32[]{:S(2)}) copy-start(f32[9,672]{1,0:T(8,128)} %np_.1) | copy-start | bytes 72580
  0.7 256.7 %copy-start.7 = (f32[9,672]{1,0:T(8,128)S(1)}, f32[9,672]{1,0:T(8,128)}, u32[]{:S(2)}) copy-start(f32[9,672]{1,0:T(8,128)} %nm.1) | copy-start | bytes 72580
  0.7 256.7 %copy-start.8 = (f32[9,672]{1,0:T(8,128)S(1)}, f32[9,672]{1,0:T(8,128)}, u32[]{:S(2)}) copy-start(f32[9,672]{1,0:T(8,128)} %nv.1) | copy-start | bytes 72580

commit v15 on v14

--- a/solution.py
+++ b/solution.py
@@ -25,7 +25,7 @@
 NORM_PAD = (16, 768)
 ROWS = 8
 PLANS = ((1792, 896), (2176, 512))
-INNER = (12, 44)
+INNER = (13, 44)
 CUT = 2 * min(side for side, _ in PLANS)
 SIDE_MAX = max(side for side, _ in PLANS)
 HALF_MAX = max(half for _, half in PLANS)
@@ -54,7 +54,8 @@
     xn = (z, f + 2 - 4 * x)
     yn = (z, f + 4 - 8 * y)
     zn = (1 - z, f)
-    peers = [(z, lax.rem(f + k, 8)) for k in range(1, 8)]
+    dc, dx, dy = 1 - 2 * c, 2 - 4 * x, 4 - 8 * y
+    peers = [(z, f + step) for step in (dx + dy + dc, dx + dy, dy + dc, dx + dc, dy, dx, dc)]
 
     def remote(src, dst, ssem, rsem, dev):
         return pltpu.make_async_remote_copy(src_ref=src, dst_ref=dst, send_sem=ssem, recv_sem=rsem,

time: 267 us -> 267 us (level)
  no operation moved by 1% of the time
where the time goes in v15:
time: 267 us
  Pallas kernels  266 us (100%)
    pallas_call x1, Pallas kernels, reduce_grads(): pl.pallas_call(functools.partial(reduce_kernel, counts), out_shape=(jax.S...  256 us
    pallas_call x1, Pallas kernels, adamw(): pl.pallas_call(adamw_kernel, out_shape=tuple(shapes), in_specs=[vmem] * 1...  9.95 us

profile of v15, /device:TPU:0, one launch (start us, length us, event | category | flops | bytes accessed | tf_op | source)
XLA Modules:
  0.0 267.1 jit_solution(3189702366423419564)
XLA Ops:
  0.6 0.0 copy-start
  0.7 0.0 copy-start.1
  0.7 0.0 copy-start.2
  0.7 0.0 copy-start.3
  0.7 0.0 copy-start.4
  0.7 0.0 copy-start.5
  0.7 0.0 copy-start.6
  0.7 0.0 copy-start.7
  0.7 0.0 copy-start.8
  0.7 256.4 %reduce_grads.1 = (f32[256,5376]{1,0:T(8,128)S(1)}, f32[128,5376]{1,0:T(8,128)S(1)}, f32[16,768]{1,0:T(8,128)S(1)}, f32[8,128]{1,0:T(8,128)S(1)}) custom-call(f32[2,2,2,256,5376]{4,3,2,1,0:T(8,128)} %bitcast.3, f32[2,2,2,128,5376]{4,3,2,1,0:T(8,128)} %bitcast.4, f32[9,1,5376]{2,1,0:T(1,128)} %bitcast.5), custom_call_target="tpu_custom_call" | custom-call | tf_op jit(solution)/shard_map/reduce_grads/pallas_call | solution.py:380
  257.1 0.0 copy-done
  257.1 0.0 copy-done.1
  257.1 0.0 copy-done.2
  257.1 0.0 copy-done.3
  257.1 0.0 copy-done.4
  257.2 0.0 copy-done.5
  257.2 0.0 copy-done.6
  257.2 0.0 copy-done.7
  257.2 0.0 copy-done.8
  257.2 9.9 %adamw.1 = (f32[256,5376]{1,0:T(8,128)}, f32[256,5376]{1,0:T(8,128)}, f32[256,5376]{1,0:T(8,128)}, bf16[256,5376]{1,0:T(8,128)(2,1)}, f32[128,5376]{1,0:T(8,128)...) custom-call(f32[8,128]{1,0:T(8,128)S(1)} %get-tuple-element.16.scale, ...), custom_call_target="tpu_custom_call" | custom-call | flops 41287680 | bytes 61931520 | tf_op jit(solution)/shard_map/adamw/pallas_call | solution.py:482
Async XLA Ops:
  0.6 256.5 %copy-start = (f32[256,5376]{1,0:T(8,128)S(1)}, f32[256,5376]{1,0:T(8,128)}, u32[]{:S(2)}) copy-start(f32[256,5376]{1,0:T(8,128)} %ep.1) | copy-start | bytes 16515076
  0.7 256.5 %copy-start.1 = (f32[256,5376]{1,0:T(8,128)S(1)}, f32[256,5376]{1,0:T(8,128)}, u32[]{:S(2)}) copy-start(f32[256,5376]{1,0:T(8,128)} %em.1) | copy-start | bytes 16515076
  0.7 256.5 %copy-start.2 = (f32[256,5376]{1,0:T(8,128)S(1)}, f32[256,5376]{1,0:T(8,128)}, u32[]{:S(2)}) copy-start(f32[256,5376]{1,0:T(8,128)} %ev.1) | copy-start | bytes 16515076
  0.7 256.5 %copy-start.3 = (f32[128,5376]{1,0:T(8,128)S(1)}, f32[128,5376]{1,0:T(8,128)}, u32[]{:S(2)}) copy-start(f32[128,5376]{1,0:T(8,128)} %mp.1) | copy-start | bytes 8257540
  0.7 256.5 %copy-start.4 = (f32[128,5376]{1,0:T(8,128)S(1)}, f32[128,5376]{1,0:T(8,128)}, u32[]{:S(2)}) copy-start(f32[128,5376]{1,0:T(8,128)} %mm.1) | copy-start | bytes 8257540
  0.7 256.5 %copy-start.5 = (f32[128,5376]{1,0:T(8,128)S(1)}, f32[128,5376]{1,0:T(8,128)}, u32[]{:S(2)}) copy-start(f32[128,5376]{1,0:T(8,128)} %mv.1) | copy-start | bytes 8257540
  0.7 256.5 %copy-start.6 = (f32[9,672]{1,0:T(8,128)S(1)}, f32[9,672]{1,0:T(8,128)}, u32[]{:S(2)}) copy-start(f32[9,672]{1,0:T(8,128)} %np_.1) | copy-start | bytes 72580
  0.7 256.5 %copy-start.7 = (f32[9,672]{1,0:T(8,128)S(1)}, f32[9,672]{1,0:T(8,128)}, u32[]{:S(2)}) copy-start(f32[9,672]{1,0:T(8,128)} %nm.1) | copy-start | bytes 72580
  0.7 256.5 %copy-start.8 = (f32[9,672]{1,0:T(8,128)S(1)}, f32[9,672]{1,0:T(8,128)}, u32[]{:S(2)}) copy-start(f32[9,672]{1,0:T(8,128)} %nv.1) | copy-start | bytes 72580

commit v16 on v15

--- a/solution.py
+++ b/solution.py
@@ -25,7 +25,7 @@
 NORM_PAD = (16, 768)
 ROWS = 8
 PLANS = ((1792, 896), (2176, 512))
-INNER = (13, 44)
+INNER = (14, 45)
 CUT = 2 * min(side for side, _ in PLANS)
 SIDE_MAX = max(side for side, _ in PLANS)
 HALF_MAX = max(half for _, half in PLANS)

time: 267 us -> 267 us (level)
  no operation moved by 1% of the time
where the time goes in v16:
time: 267 us
  Pallas kernels  266 us (100%)
    pallas_call x1, Pallas kernels, reduce_grads(): pl.pallas_call(functools.partial(reduce_kernel, counts), out_shape=(jax.S...  256 us
    pallas_call x1, Pallas kernels, adamw(): pl.pallas_call(adamw_kernel, out_shape=tuple(shapes), in_specs=[vmem] * 1...  9.95 us

profile of v16, /device:TPU:0, one launch (start us, length us, event | category | flops | bytes accessed | tf_op | source)
XLA Modules:
  0.0 267.0 jit_solution(541035850412424418)
XLA Ops:
  0.6 0.0 copy-start
  0.7 0.0 copy-start.1
  0.7 0.0 copy-start.2
  0.7 0.0 copy-start.3
  0.7 0.0 copy-start.4
  0.7 0.0 copy-start.5
  0.7 0.0 copy-start.6
  0.7 0.0 copy-start.7
  0.7 0.0 copy-start.8
  0.7 256.2 %reduce_grads.1 = (f32[256,5376]{1,0:T(8,128)S(1)}, f32[128,5376]{1,0:T(8,128)S(1)}, f32[16,768]{1,0:T(8,128)S(1)}, f32[8,128]{1,0:T(8,128)S(1)}) custom-call(f32[2,2,2,256,5376]{4,3,2,1,0:T(8,128)} %bitcast.3, f32[2,2,2,128,5376]{4,3,2,1,0:T(8,128)} %bitcast.4, f32[9,1,5376]{2,1,0:T(1,128)} %bitcast.5), custom_call_target="tpu_custom_call" | custom-call | tf_op jit(solution)/shard_map/reduce_grads/pallas_call | solution.py:380
  256.9 0.0 copy-done
  256.9 0.0 copy-done.1
  256.9 0.0 copy-done.2
  257.0 0.0 copy-done.3
  257.0 0.0 copy-done.4
  257.0 0.0 copy-done.5
  257.0 0.0 copy-done.6
  257.0 0.0 copy-done.7
  257.0 0.0 copy-done.8
  257.0 9.9 %adamw.1 = (f32[256,5376]{1,0:T(8,128)}, f32[256,5376]{1,0:T(8,128)}, f32[256,5376]{1,0:T(8,128)}, bf16[256,5376]{1,0:T(8,128)(2,1)}, f32[128,5376]{1,0:T(8,128)...) custom-call(f32[8,128]{1,0:T(8,128)S(1)} %get-tuple-element.16.scale, ...), custom_call_target="tpu_custom_call" | custom-call | flops 41287680 | bytes 61931520 | tf_op jit(solution)/shard_map/adamw/pallas_call | solution.py:482
Async XLA Ops:
  0.6 256.3 %copy-start = (f32[256,5376]{1,0:T(8,128)S(1)}, f32[256,5376]{1,0:T(8,128)}, u32[]{:S(2)}) copy-start(f32[256,5376]{1,0:T(8,128)} %ep.1) | copy-start | bytes 16515076
  0.7 256.3 %copy-start.1 = (f32[256,5376]{1,0:T(8,128)S(1)}, f32[256,5376]{1,0:T(8,128)}, u32[]{:S(2)}) copy-start(f32[256,5376]{1,0:T(8,128)} %em.1) | copy-start | bytes 16515076
  0.7 256.3 %copy-start.2 = (f32[256,5376]{1,0:T(8,128)S(1)}, f32[256,5376]{1,0:T(8,128)}, u32[]{:S(2)}) copy-start(f32[256,5376]{1,0:T(8,128)} %ev.1) | copy-start | bytes 16515076
  0.7 256.3 %copy-start.3 = (f32[128,5376]{1,0:T(8,128)S(1)}, f32[128,5376]{1,0:T(8,128)}, u32[]{:S(2)}) copy-start(f32[128,5376]{1,0:T(8,128)} %mp.1) | copy-start | bytes 8257540
  0.7 256.3 %copy-start.4 = (f32[128,5376]{1,0:T(8,128)S(1)}, f32[128,5376]{1,0:T(8,128)}, u32[]{:S(2)}) copy-start(f32[128,5376]{1,0:T(8,128)} %mm.1) | copy-start | bytes 8257540
  0.7 256.3 %copy-start.5 = (f32[128,5376]{1,0:T(8,128)S(1)}, f32[128,5376]{1,0:T(8,128)}, u32[]{:S(2)}) copy-start(f32[128,5376]{1,0:T(8,128)} %mv.1) | copy-start | bytes 8257540
  0.7 256.3 %copy-start.6 = (f32[9,672]{1,0:T(8,128)S(1)}, f32[9,672]{1,0:T(8,128)}, u32[]{:S(2)}) copy-start(f32[9,672]{1,0:T(8,128)} %np_.1) | copy-start | bytes 72580
  0.7 256.3 %copy-start.7 = (f32[9,672]{1,0:T(8,128)S(1)}, f32[9,672]{1,0:T(8,128)}, u32[]{:S(2)}) copy-start(f32[9,672]{1,0:T(8,128)} %nm.1) | copy-start | bytes 72580
  0.7 256.3 %copy-start.8 = (f32[9,672]{1,0:T(8,128)S(1)}, f32[9,672]{1,0:T(8,128)}, u32[]{:S(2)}) copy-start(f32[9,672]{1,0:T(8,128)} %nv.1) | copy-start | bytes 72580
